TPU v7x, 256 devices: a whole 4x4x8 slice. The times are simulated.
256 devices in a mesh: dp: 16 (over y_hi, x, core), mp: 16 (over z, y_lo).
Axes of the slice: x: 4, y: 4 (y_hi: 2, y_lo: 2; y = y_hi * 2 + y_lo), z: 8, core: 2. Of those that a mesh axis runs over, the one named last changes fastest.
Arguments:
- tokens: bfloat16 [8192, 8192], P(('dp', 'mp')), parts along dimension 0, may hold values from -6 to 6
- norm_gain: float32 [8192], replicated, may hold values from 0.5 to 1.5
- qkv_weight: bfloat16 [8192, 10240], P(None, 'mp'), may hold values from -0.0625 to 0.0625
- qkv_bias: float32 [10240], P('mp'), may hold values from -3 to 3
- qkv_grad: bfloat16 [8192, 10240], P('dp', 'mp'), parts along dimension 0, may hold values from -6 to 6
Outputs:
- qkv: bfloat16 [8192, 10240], P('dp', 'mp'), parts along dimension 0
- tokens_grad: float32 [8192, 8192], P(('dp', 'mp')), parts along dimension 0
- gain_grad: float32 [131072], P('dp'), parts along dimension 0
- bias_grad: float32 [163840], P(('dp', 'mp')), parts along dimension 0
There are 16 independent parts, one for each index of `dp`. A program takes and returns all parts, laid end to end along the dimension named above; an argument that names none is the same for every part. Nothing has to cross between parts.
All inputs are finite; a program needn't handle non-finite values.
Results may differ from a plain program's by a relative error of at most 0.0046.
Values may be sent and summed in bfloat16 or wider, within the bound.
A program may use at most 128 MiB of HBM per device.

v0:
```python
import jax
import jax.numpy as jnp
from jax import lax
from jax.sharding import Mesh
from jax.sharding import PartitionSpec as P

HEAD_DIM = 128
SEQ_LEN = 32768
GROUP = 10
TOK_DEV = 32
MP = ("mp_0", "mp_1")
DP_MP = ("dp", "mp_0", "mp_1")


def summed_rows(total, axes):
    for axis in axes:
        total = lax.psum_scatter(total, axis, scatter_dimension=0, tiled=True)
    return total


def over_axes(value, axes):
    for axis in axes:
        value = lax.psum(value, axis)
    return value


def rotate_heads(joined, first_col, position, sign):
    rows, cols = joined.shape
    heads = cols // HEAD_DIM
    half = HEAD_DIM // 2
    parts = joined.reshape(rows, heads, 2, half)
    inverse = jnp.exp(
        -jnp.log(jnp.float32(1000000.0)) * (2.0 * jnp.arange(half).astype(jnp.float32) / HEAD_DIM)
    )
    angle = position.astype(jnp.float32)[:, None] * inverse[None, :]
    cosine = jnp.cos(angle)[:, None, :]
    sine = sign * jnp.sin(angle)[:, None, :]
    first = parts[:, :, 0, :]
    second = parts[:, :, 1, :]
    turned = jnp.stack([first * cosine - second * sine, second * cosine + first * sine], axis=2)
    head_index = first_col // HEAD_DIM + jnp.arange(heads)
    rotated = head_index % GROUP != GROUP - 1
    result = jnp.where(rotated[None, :, None, None], turned, parts)
    return result.reshape(rows, cols)


def positions(rows, stride):
    row_index = jnp.arange(rows)
    return row_index // TOK_DEV * stride + row_index % TOK_DEV


def normalize(tokens, norm_gain):
    values = tokens.astype(jnp.float32)
    scale = lax.rsqrt(jnp.mean(values * values, axis=1, keepdims=True) + 1e-06)
    return (values * scale * norm_gain[None, :]).astype(jnp.bfloat16)


def shards(tokens, norm_gain, qkv_weight, qkv_bias, qkv_grad):
    width = qkv_weight.shape[1]
    first_col = lax.axis_index(MP) * width
    stride = SEQ_LEN // lax.axis_size(MP)
    place = positions(qkv_grad.shape[0], stride)
    joined_grad = rotate_heads(qkv_grad.astype(jnp.float32), first_col, place, -1.0)
    bias_grad = jnp.sum(joined_grad, axis=0)
    joined_low = joined_grad.astype(jnp.bfloat16)
    normed_grad = summed_rows(
        lax.dot_general(
            joined_low, qkv_weight, (((1,), (1,)), ((), ())), preferred_element_type=jnp.float32
        ),
        MP,
    )
    values = tokens.astype(jnp.float32)
    scale = lax.rsqrt(jnp.mean(values * values, axis=1, keepdims=True) + 1e-06)
    gain_grad = over_axes(jnp.sum(normed_grad * values * scale, axis=0), MP)
    inner = jnp.mean(norm_gain[None, :] * normed_grad * values, axis=1, keepdims=True)
    tokens_grad = scale * norm_gain[None, :] * normed_grad - values * scale * scale * scale * inner
    tokens_grad, gain_grad, bias_grad = (tokens_grad, gain_grad, bias_grad)
    tokens_grad, later = lax.optimization_barrier((tokens_grad, tokens))
    normed = normalize(later, norm_gain)
    project_normed = lax.all_gather(normed, MP, axis=0, tiled=True)
    joined = (
        jnp.dot(project_normed, qkv_weight, preferred_element_type=jnp.float32) + qkv_bias[None, :]
    )
    place = positions(project_normed.shape[0], stride)
    qkv = rotate_heads(joined, first_col, place, 1.0).astype(jnp.bfloat16)
    return (qkv, tokens_grad, gain_grad, bias_grad)


def solution(mesh):
    split = Mesh(mesh.devices.reshape(mesh.shape["dp"], 8, 2), ("dp", "mp_0", "mp_1"))
    placed = (P(DP_MP, None), P(), P(None, MP), P(MP), P("dp", MP))
    return jax.shard_map(
        shards,
        mesh=split,
        in_specs=placed,
        out_specs=(P("dp", MP), P(DP_MP, None), P("dp"), P(DP_MP)),
        check_vma=False,
    )
```

profile of v0, /device:TPU:4, one launch (start us, length us, event | category | flops | bytes accessed | tf_op | source)
XLA Modules:
  0.0 452.4 jit_solution(2797563388790538851)
XLA Ops:
  7.4 0.1 broadcast_in_dim.16
  7.4 1.3 copy.9
  8.8 0.5 multiply_sine_fusion
  9.3 0.2 multiply_subtract_fusion.1
  9.5 0.1 pad_maximum_fusion
  9.6 0.4 copy.10
  10.0 0.7 copy-done.2
  10.7 14.1 %fusion.11 = f32[512,8192]{1,0:T(8,128)} fusion(bf16[8192,640]{1,0:T(8,128)(2,1)} %param.7, f32[512,640]{1,0:T(8,128)S(1)} %copy.10, pred[640]{0:T(1024)(128)(4,1)S(1)} %broadcast_in_dim.16, bf16[512,640]{1,0:T(8,128)(2,1)S(1)} %copy-done.2), kind=kOutput, calls=%fused_computation.23 | convolution fusion | flops 5369364480 | bytes 29229696 | tf_op jit(solution)/shard_map/dot_general | solution.py:67
  24.9 176.6 %reduce-scatter.3.cloned.1.call-done = f32[64,8192]{1,0:T(8,128)} async-done(((f32[512,8192]{1,0:T(8,128)}), f32[64,8192]{1,0:T(8,128)}) %reduce-scatter.3.cloned.1.call-update) | async-done | bytes 2097168 | tf_op jit(solution)/shard_map/reduce_scatter | solution.py:17
  201.6 0.2 fusion.3
  201.8 37.8 %reduce-scatter.5.cloned.1.call-done = f32[32,8192]{1,0:T(8,128)} async-done(((f32[64,8192]{1,0:T(8,128)}), f32[32,8192]{1,0:T(8,128)}) %reduce-scatter.5.cloned.1.call-update) | async-done | bytes 1048592 | tf_op jit(solution)/shard_map/reduce_scatter | solution.py:17
  239.7 1.7 fusion.10
  241.4 1.3 fusion.7
  242.7 0.2 fusion
  243.0 1.0 fusion.2
  244.0 0.8 fusion.13
  244.8 30.3 %psum.14 = f32[8192]{0:T(1024)S(1)} all-reduce(f32[8192]{0:T(1024)S(1)} %get-tuple-element.8), channel_id=1, replica_groups=mesh['dp'=16,'mp_0'=8,'mp_1'=2] {'mp_0'}, use_global_device_ids=true, to_apply=%region_6.7 | all-reduce | flops 8192 | bytes 65536 | tf_op jit(solution)/shard_map/psum | solution.py:23
  275.1 10.9 %psum.15 = f32[8192]{0:T(1024)} all-reduce(f32[8192]{0:T(1024)S(1)} %psum.14), channel_id=1, replica_groups=mesh['dp'=16,'mp_0'=8,'mp_1'=2] {'mp_1'}, use_global_device_ids=true, to_apply=%region_7.8 | all-reduce | flops 8192 | bytes 65536 | tf_op jit(solution)/shard_map/psum | solution.py:23
  286.0 142.3 %all-gather.2.cloned.1.call-done = bf16[512,8192]{1,0:T(8,128)(2,1)} async-done(((bf16[32,8192]{1,0:T(8,128)(2,1)}), bf16[512,8192]{1,0:T(8,128)(2,1)}) %all-gather.2.cloned.1.call-update) | async-done | bytes 8388624 | tf_op jit(solution)/shard_map/all_gather | solution.py:80
  428.3 15.7 %convolution_add_fusion = f32[512,640]{1,0:T(8,128)S(1)} fusion(bf16[512,8192]{1,0:T(8,128)(2,1)} %all-gather.2.cloned.1.call-done, bf16[8192,640]{1,0:T(8,128)(2,1)} %param.7, f32[640]{0:T(1024)S(1)} %copy-done.4), kind=kOutput, calls=%fused_computation.4 | convolution fusion | flops 5369036800 | bytes 20187648 | tf_op jit(solution)/shard_map/dot_general | solution.py:82
  443.9 0.4 copy.11
  444.3 0.2 multiply_subtract_fusion
  444.7 0.3 copy.12
  445.0 1.0 select_convert_fusion
  (23 shorter events, 0.4 us)
Async XLA Ops:
  7.2 194.3 %reduce-scatter.3.cloned.1.call-start = ((), (), s32[]{:S(2)}) async-start(), calls=%async_computation.2 | async-start | bytes 18874368 | tf_op jit(solution)/shard_map/reduce_scatter | solution.py:17
  9.6 1.1 copy-start.2
  24.9 176.7 %copy-start = (bf16[32,8192]{1,0:T(8,128)(2,1)S(1)}, bf16[32,8192]{1,0:T(8,128)(2,1)}, u32[]{:S(2)}) copy-start(bf16[32,8192]{1,0:T(8,128)(2,1)} %param.5) | copy-start | bytes 1572868
  24.9 214.8 %reduce-scatter.5.cloned.1.call-start = ((), (), s32[]{:S(2)}) async-start(), calls=%async_computation.3 | async-start | bytes 3145728 | tf_op jit(solution)/shard_map/reduce_scatter | solution.py:17
  201.5 38.2 %copy-start.3 = (f32[8192]{0:T(1024)S(1)}, f32[8192]{0:T(1024)}, u32[]{:S(2)}) copy-start(f32[8192]{0:T(1024)} %param.6) | copy-start | bytes 98308
  201.5 226.7 %all-gather.2.cloned.1.call-start = ((), (), s32[]{:S(2)}) async-start(), calls=%async_computation.4 | async-start | bytes 8912896 | tf_op jit(solution)/shard_map/all_gather | solution.py:80
  239.7 1.7 copy-start.1
  244.0 184.3 %copy-start.4 = (f32[640]{0:T(1024)S(1)}, f32[640]{0:T(1024)}, u32[]{:S(2)}) copy-start(f32[640]{0:T(1024)} %param.8) | copy-start | bytes 7684
Sparse Core Ops, SparseCore 0:
  25.0 176.4 reduce-scatter.2
  204.0 35.6 reduce-scatter.4
  244.1 184.1 all-gather.1
where the time goes:
time: 454 us; the launch traced here: 452 us
  waiting for transfers between devices  357 us (79%)
  blocking collectives  41.2 us (9%)
  matrix products  29.8 us (7%)
  between operations  13.9 us (3%)
  other arithmetic  7.41 us (2%)
    reduce_scatter x2, waiting for transfers between devices, summed_rows(): total = lax.psum_scatter(total, axis, scatter_dimension=0, tiled=True)  214 us
    all_gather x1, waiting for transfers between devices, shards(): project_normed = lax.all_gather(normed, MP, axis=0, tiled=True)  142 us
    psum x2, blocking collectives, over_axes(): value = lax.psum(value, axis)  41.2 us
    dot_general x1, matrix products, shards(): jnp.dot(project_normed, qkv_weight, preferred_element_type=jnp.float32)  15.7 us
    dot_general x1, matrix products, shards(): lax.dot_general(joined_low, qkv_weight, (((1,), (1,)), ((), ())), preferr...  14.1 us
  transfers between devices with their start and end apart: 3, of which 3 were waited for; matrix products, arithmetic and copies ran while one was open for 0% of the time, Pallas kernels for 0%

commit v1 on v0

v1 whole, which is shorter than its diff:
```python
import functools

import jax
import jax.numpy as jnp
import numpy as np
from jax import lax
from jax.experimental import pallas as pl
from jax.experimental.pallas import tpu as pltpu
from jax.sharding import Mesh
from jax.sharding import PartitionSpec as P

HEAD = 128
SEQ_LEN = 32768
MESH = pl.DeviceIdType.MESH
AXES = ("yh", "x", "core", "z", "yl")
Z = 8
N = 8
PER = 7
f32 = jnp.float32
bf16 = jnp.bfloat16


def rcopy(src, dst, ssem, rsem, **where):
    return pltpu.make_async_remote_copy(
        src_ref=src, dst_ref=dst, send_sem=ssem, recv_sem=rsem, device_id=where, device_id_type=MESH
    )


def kernel(
    tok_h, w_h, qg_h, gain_h, bias_h, cos_h, sin_h,
    qkv_o, tg_o, gg_o, bg_o,
    w, tok, nrm, part, rb, sb, qb, qp, jl, out, ng, scl, inner, acc,
    gp, gr, gs, gy, gf, gain, bias, bgv, cosv, sinv,
    ag_r, ag_s, w_r, w_s, d_r, d_s, rs_r, rs_s, q_r, q_s, b_r, b_s, o_r, o_s,
    g_r, g_s, gy_r, gy_s, gf_r, gf_s, loc,
):
    rows, dim = tok_h.shape
    width = w_h.shape[1]
    F = dim // N
    H = F // 2
    half = dim // 2
    yh, core, z, yl = (lax.axis_index(a) for a in ("yh", "core", "z", "yl"))

    def zz(k):
        return lax.rem(z + (k + Z), Z)

    direct = {"yl": 1 - yl}
    other = {"yh": 1 - yh, "yl": 1 - yl}
    sibling = {"core": 1 - core}
    own = pl.ds(pl.multiple_of(yl * width, 128), width)
    far = pl.ds(pl.multiple_of((1 - yl) * width, 128), width)

    local = [
        pltpu.make_async_copy(tok_h, tok.at[z], loc.at[0]),
        pltpu.make_async_copy(qg_h, qb, loc.at[1]),
        pltpu.make_async_copy(cos_h, cosv, loc.at[2]),
        pltpu.make_async_copy(sin_h, sinv, loc.at[3]),
        pltpu.make_async_copy(gain_h, gain, loc.at[4]),
        pltpu.make_async_copy(bias_h, bias.at[:, own], loc.at[5]),
        pltpu.make_async_copy(w_h, w.at[:, own], loc.at[6]),
    ]
    for copy in local:
        copy.start()

    barrier = pltpu.get_barrier_semaphore()
    for k in range(1, Z):
        pl.semaphore_signal(barrier, inc=1, device_id={"z": zz(k)}, device_id_type=MESH)
    for where in (direct, other, sibling):
        pl.semaphore_signal(barrier, inc=1, device_id=where, device_id_type=MESH)
    pl.semaphore_wait(barrier, Z + 2)

    def ag_half(d, k):
        return d if k % 2 == 0 else 1 - d

    def ag_copy(d, k):
        step = k // 2
        block = zz(-step) if d == 0 else zz(step)
        cols = pl.ds(ag_half(d, k) * half, half)
        src = tok_h.at[:, cols] if step == 0 else tok.at[block, :, cols]
        return rcopy(src, tok.at[block, :, cols], ag_s.at[d, k], ag_r.at[d, k], z=zz(1 if d == 0 else -1))

    for k in range(2):
        for d in range(2):
            ag_copy(d, k).start()

    q_copy = rcopy(qg_h.at[:, 1 - yl], qp, q_s.at[0], q_r.at[0], **direct)
    q_copy.start()
    b_copy = rcopy(bias_h, bias.at[:, own], b_s.at[0], b_r.at[0], **direct)
    b_copy.start()

    share = F // 2
    piece = share // 2

    def w_copy(j, s):
        at = pl.ds(pl.multiple_of(j * F + core * share + s * piece, piece), piece)
        return rcopy(w_h.at[at], w.at[at, own], w_s.at[s, j], w_r.at[s, j], **(direct if s == 0 else other))

    def w_got(j, s):
        at = pl.ds(pl.multiple_of(j * F + core * share + s * piece, piece), piece)
        return rcopy(w.at[at, far], w.at[at, far], w_s.at[s, j], w_r.at[s, j], **(direct if s == 0 else other))

    def d_copy(j):
        at = pl.ds(pl.multiple_of(j * F + core * share, share), share)
        return rcopy(w.at[at, far], w.at[at, far], d_s.at[j], d_r.at[j], **sibling)

    def d_got(j):
        at = pl.ds(pl.multiple_of(j * F + (1 - core) * share, share), share)
        return rcopy(w.at[at, far], w.at[at, far], d_s.at[j], d_r.at[j], **sibling)

    def hand_on(j):
        w_got(j, 0).wait_recv()
        w_got(j, 1).wait_recv()
        d_copy(j).start()

    for j in range(N):
        w_copy(j, 0).start()
        w_copy(j, 1).start()

    def norm_block(b):
        step = min(512, dim)

        def sq(i, total):
            v = tok[b, :, pl.ds(pl.multiple_of(i * step, step), step)].astype(f32)
            v = v * v
            for q in range(step // 128):
                total = total + v[:, q * 128:(q + 1) * 128]
            return total

        total = lax.fori_loop(0, dim // step, sq, jnp.zeros((rows, 128), f32))
        mean = jnp.sum(total, axis=1, keepdims=True) / dim
        s = jnp.broadcast_to(lax.rsqrt(mean + 1e-06), (rows, 128))
        scl[b] = s
        wide = jnp.concatenate([s] * (step // 128), axis=1)

        def put(i, carry):
            at = pl.ds(pl.multiple_of(i * step, step), step)
            v = tok[b, :, at].astype(f32)
            nrm[b, :, at] = (v * wide * gain[:, at]).astype(bf16)
            return carry

        lax.fori_loop(0, dim // step, put, 0)

    def turn_back(x, line, b, is_value):
        c = cosv[line, pl.ds(pl.multiple_of(b * rows, rows), rows), :]
        s = sinv[line, pl.ds(pl.multiple_of(b * rows, rows), rows), :]
        r = x * c - pltpu.roll(x, HEAD // 2, 1) * s
        return r if is_value is None else jnp.where(is_value, x, r)

    heads = width // HEAD

    def own_columns():
        bgv[...] = jnp.zeros_like(bgv)

        def one(b, carry):
            at = pl.ds(pl.multiple_of(b * rows, rows), rows)
            for h in range(heads):
                value = (yl == 1) if h == heads - 1 else None
                hs = pl.ds(h * HEAD, HEAD)
                for line in range(2):
                    r = turn_back(qb[b, line, :, hs].astype(f32), line, b, value)
                    bgv[:, hs] += jnp.sum(r, axis=0, keepdims=True)
                r = turn_back(qb[b, yl, :, hs].astype(f32), yl, b, value)
                jl[at, pl.ds(pl.multiple_of(yl * width + h * HEAD, HEAD), HEAD)] = r.astype(bf16)
            return carry

        lax.fori_loop(0, Z, one, 0)

    def far_columns():
        def one(b, carry):
            at = pl.ds(pl.multiple_of(b * rows, rows), rows)
            for h in range(heads):
                value = (yl == 0) if h == heads - 1 else None
                r = turn_back(qp[b, :, pl.ds(h * HEAD, HEAD)].astype(f32), yl, b, value)
                jl[at, pl.ds(pl.multiple_of((1 - yl) * width + h * HEAD, HEAD), HEAD)] = r.astype(bf16)
            return carry

        lax.fori_loop(0, Z, one, 0)

    for k in range(1, 5):
        local[k].wait()
    own_columns()
    local[0].wait()
    norm_block(z)
    local[5].wait()
    bg_copy = pltpu.make_async_copy(bgv, bg_o, loc.at[7])
    bg_copy.start()

    for k in range(PER):
        for d in range(2):
            block = zz(-1 - k // 2) if d == 0 else zz(1 + k // 2)
            cols = pl.ds(ag_half(d, k) * half, half)
            spot = tok.at[block, :, cols]
            rcopy(spot, spot, ag_s.at[d, k], ag_r.at[d, k], z=z).wait_recv()
            if k + 2 < PER:
                ag_copy(d, k + 2).start()
        if k == 1:
            q_copy.wait_recv()
            b_copy.wait_recv()
            far_columns()
        if k % 2 == 1:
            norm_block(zz(-1 - k // 2))
            norm_block(zz(1 + k // 2))
        if k == 6:
            norm_block(zz(4))
        if 4 <= k:
            hand_on(k - 4)
    local[6].wait()

    bt = min(256, F)

    def backward_chunk(c):
        @pl.when(c < 6)
        def _():
            d_got(c).wait_recv()

        def one(t, carry):
            at = pl.ds(pl.multiple_of(c * F + t * bt, bt), bt)
            got = lax.dot_general(jl[...], w[at, :], (((1,), (1,)), ((), ())), preferred_element_type=f32)
            part[:, :, at] = got.reshape(Z, rows, bt)
            return carry

        lax.fori_loop(0, F // bt, one, 0)

    def span(c, hf):
        return pl.ds(pl.multiple_of(c * F + hf * H, H), H)

    def rs_copy(d, c, slot, src):
        return rcopy(src, rb.at[d, c, slot], rs_s.at[d, c, slot], rs_r.at[d, c, slot], z=zz(1 if d == 0 else -1))

    def first_hop(c):
        for d in range(2):
            for short in range(2):
                hf = d if short == 0 else 1 - d
                dist = 4 - short
                sb[d, c, short] = part[zz(dist if d == 0 else -dist), :, span(c, hf)].astype(bf16)
                rs_copy(d, c, 4 * short, sb.at[d, c, short]).start()

    def later_hop(c, hop):
        for d in range(2):
            for short in range(2):
                if short and hop == 4:
                    continue
                hf = d if short == 0 else 1 - d
                dist = 5 - hop - short
                slot = 4 * short + hop - 2
                rs_copy(d, c, slot, rb.at[d, c, slot]).wait_recv()
                mine = part[zz(dist if d == 0 else -dist), :, span(c, hf)]
                rb[d, c, slot] = (rb[d, c, slot].astype(f32) + mine).astype(bf16)
                rs_copy(d, c, slot + 1, rb.at[d, c, slot]).start()

    def finish(c):
        for d in range(2):
            rs_copy(d, c, 3, rb.at[d, c, 3]).wait_recv()
            rs_copy(d, c, 6, rb.at[d, c, 6]).wait_recv()
        total = inner[...]
        for hf in range(2):
            at = span(c, hf)
            got = part[z, :, at] + rb[hf, c, 3].astype(f32) + rb[1 - hf, c, 6].astype(f32)
            ng[:, at] = got
            t = got * gain[:, at] * tok[z, :, at].astype(f32)
            for q in range(H // 128):
                total = total + t[:, q * 128:(q + 1) * 128]
        inner[...] = total

    def gain_part(c):
        def one(t, carry):
            at = pl.ds(pl.multiple_of(c * F + t * 128, 128), 128)
            total = jnp.zeros((rows, 128), f32)
            for b in range(Z):
                total = total + part[b, :, at] * tok[b, :, at].astype(f32) * scl[b]
            gp[c, :, pl.ds(pl.multiple_of(t * 128, 128), 128)] = jnp.sum(total, axis=0, keepdims=True)
            return carry

        lax.fori_loop(0, F // 128, one, 0)

    def g_send(c):
        return rcopy(gp.at[c], gr.at[z], g_s.at[c], g_r.at[z], z=c)

    def gf_send(k):
        return rcopy(gf.at[z], gf.at[z], gf_s.at[k], gf_r.at[z], z=zz(k))

    gy_copy = rcopy(gs, gy, gy_s.at[0], gy_r.at[0], **direct)

    def forward_tile(t):
        n = jnp.where(yl == 0, t, 4 - t)
        cols = pl.ds(pl.multiple_of(n * 256, 256), 256)
        deep = dim // 4
        acc[...] = jnp.broadcast_to(bias[:, cols], acc.shape)

        def one(k, carry):
            at = pl.ds(pl.multiple_of(k * deep, deep), deep)
            lhs = nrm[:, :, at].reshape(Z * rows, deep)
            acc[...] += jnp.dot(lhs, w[at, cols], preferred_element_type=f32)
            return carry

        lax.fori_loop(0, 4, one, 0)

        def spin(b, carry):
            at = pl.ds(pl.multiple_of(b * rows, rows), rows)
            for h in range(2):
                x = acc[at, h * HEAD:(h + 1) * HEAD]
                r = x * cosv[yl, at, :] + pltpu.roll(x, HEAD // 2, 1) * sinv[yl, at, :]
                if h == 1:
                    r = jnp.where(n == 4, x, r)
                out[b, :, pl.ds(pl.multiple_of(n * 256 + h * HEAD, HEAD), HEAD)] = r.astype(bf16)
            return carry

        lax.fori_loop(0, Z, spin, 0)

    o_copy = rcopy(out.at[:, :, far], qkv_o.at[:, yl], o_s.at[0], o_r.at[0], **direct)
    o_local = pltpu.make_async_copy(out.at[:, :, own], qkv_o.at[:, yl], loc.at[8])

    inner[...] = jnp.zeros_like(inner)

    def iteration(i, carry):
        @pl.when(i < N)
        def _():
            backward_chunk(i)
            first_hop(i)

        for hop in (2, 3, 4):
            @pl.when((i >= hop - 1) & (i < N + hop - 1))
            def _(hop=hop):
                later_hop(i - hop + 1, hop)

        @pl.when(i >= 4)
        def _():
            finish(i - 4)

        @pl.when(i < N)
        def _():
            gain_part(i)

            @pl.when(i != z)
            def _():
                g_send(i).start()

        @pl.when(i == z + 1)
        def _():
            total = gp[z]
            for k in range(1, Z):
                spot = gr.at[zz(k)]
                rcopy(spot, spot, g_s.at[zz(k)], g_r.at[zz(k)], z=z).wait_recv()
                total = total + gr[zz(k)]
            gs[...] = total
            gy_copy.start()

        @pl.when(i == z + 2)
        def _():
            gy_copy.wait_recv()
            gf[z] = gs[...] + gy[...]
            for k in range(1, Z):
                gf_send(k).start()

        @pl.when(i < 3)
        def _():
            hand_on(i + 3)

        @pl.when((i == 4) | (i == 5))
        def _():
            hand_on(i + 2)

        @pl.when((i < 2) | ((i >= 5) & (i < 8)))
        def _():
            @pl.when(i == 5)
            def _():
                d_got(6).wait_recv()
                d_got(7).wait_recv()
            forward_tile(jnp.where(i < 2, i, i - 3))

        @pl.when(i == 7)
        def _():
            o_copy.start()
            o_local.start()
        return carry

    lax.fori_loop(0, N + 4, iteration, 0)

    mean = jnp.sum(inner[...], axis=1, keepdims=True) / dim
    s = scl[z]
    k3 = s * s * s * jnp.broadcast_to(mean, s.shape)
    s4 = jnp.concatenate([s] * 4, axis=1)
    k4 = jnp.concatenate([k3] * 4, axis=1)

    def last(i, carry):
        at = pl.ds(pl.multiple_of(i * 512, 512), 512)
        ng[:, at] = s4 * gain[:, at] * ng[:, at] - tok[z, :, at].astype(f32) * k4
        return carry

    outs = []
    for q in range(4):
        per = dim // 2048
        lax.fori_loop(q * per, (q + 1) * per, last, 0)
        at = pl.ds(q * (dim // 4), dim // 4)
        copy = pltpu.make_async_copy(ng.at[:, at], tg_o.at[:, at], loc.at[9 + q])
        copy.start()
        outs.append(copy)

    for k in range(1, Z):
        spot = gf.at[zz(k)]
        rcopy(spot, spot, gf_s.at[k], gf_r.at[zz(k)], z=z).wait_recv()
    g_out = pltpu.make_async_copy(gf, gg_o, loc.at[13])
    g_out.start()

    for d in range(2):
        for k in range(PER):
            ag_copy(d, k).wait_send()
    q_copy.wait_send()
    b_copy.wait_send()
    gy_copy.wait_send()

    def sent(c, carry):
        w_copy(c, 0).wait_send()
        w_copy(c, 1).wait_send()
        d_copy(c).wait_send()
        for d in range(2):
            for slot in range(PER):
                rs_copy(d, c, slot, rb.at[d, c, slot]).wait_send()

        @pl.when(c != z)
        def _():
            g_send(c).wait_send()
        return carry

    lax.fori_loop(0, N, sent, 0)
    for k in range(1, Z):
        gf_send(k).wait_send()
    o_copy.wait()
    o_local.wait()
    bg_copy.wait()
    g_out.wait()
    for copy in outs:
        copy.wait()


def tables(tokens_per):
    mp = 2 * Z
    block = np.arange(mp).reshape(Z, 2).T.reshape(-1)
    position = (block[:, None] * (SEQ_LEN // mp) + np.arange(tokens_per)[None, :]).reshape(-1)
    half = HEAD // 2
    inverse = np.exp(-np.log(1000000.0) * (2.0 * np.arange(half) / HEAD))
    angle = position[:, None].astype(np.float64) * inverse[None, :]
    c, s = np.cos(angle), np.sin(angle)
    shape = (2, Z * tokens_per, HEAD)
    return (
        np.concatenate([c, c], axis=1).astype(np.float32).reshape(shape),
        np.concatenate([-s, s], axis=1).astype(np.float32).reshape(shape),
    )


def shards(tokens, norm_gain, qkv_weight, qkv_bias, qkv_grad):
    rows, dim = tokens.shape
    width = qkv_weight.shape[1]
    F = dim // N
    H = F // 2
    both = 2 * width
    cos, sin = tables(rows)
    any_spec = pl.BlockSpec(memory_space=pl.ANY)
    dma = pltpu.SemaphoreType.DMA
    V = pltpu.VMEM
    qkv, tokens_grad, gain_grad, bias_grad = pl.pallas_call(
        kernel,
        name="qkv_ring",
        out_shape=(
            jax.ShapeDtypeStruct((Z, 2, rows, width), bf16),
            jax.ShapeDtypeStruct((rows, dim), f32),
            jax.ShapeDtypeStruct((Z, 1, F), f32),
            jax.ShapeDtypeStruct((1, width), f32),
        ),
        in_specs=[any_spec] * 7,
        out_specs=(any_spec,) * 4,
        scratch_shapes=[
            V((dim, both), bf16),
            V((Z, rows, dim), bf16),
            V((Z, rows, dim), bf16),
            V((Z, rows, dim), f32),
            V((2, N, PER, rows, H), bf16),
            V((2, N, 2, rows, H), bf16),
            V((Z, 2, rows, width), bf16),
            V((Z, rows, width), bf16),
            V((Z * rows, both), bf16),
            V((Z, rows, both), bf16),
            V((rows, dim), f32),
            V((Z, rows, 128), f32),
            V((rows, 128), f32),
            V((Z * rows, 256), f32),
            V((N, 1, F), f32),
            V((Z, 1, F), f32),
            V((1, F), f32),
            V((1, F), f32),
            V((Z, 1, F), f32),
            V((1, dim), f32),
            V((1, both), f32),
            V((1, width), f32),
            V(cos.shape, f32),
            V(sin.shape, f32),
            dma((2, PER)), dma((2, PER)),
            dma((2, N)), dma((2, N)),
            dma((N,)), dma((N,)),
            dma((2, N, PER)), dma((2, N, PER)),
            dma((1,)), dma((1,)),
            dma((1,)), dma((1,)),
            dma((1,)), dma((1,)),
            dma((Z,)), dma((Z,)),
            dma((1,)), dma((1,)),
            dma((Z,)), dma((Z,)),
            dma((14,)),
        ],
        compiler_params=pltpu.CompilerParams(
            collective_id=0, has_side_effects=True, vmem_limit_bytes=66_000_000
        ),
    )(
        tokens,
        qkv_weight,
        qkv_grad.reshape(Z, 2, rows, width),
        norm_gain.reshape(1, dim),
        qkv_bias.reshape(1, width),
        jnp.asarray(cos),
        jnp.asarray(sin),
    )
    return (
        qkv.reshape(2 * Z * rows, width),
        tokens_grad,
        gain_grad.reshape(dim),
        bias_grad.reshape(width),
    )


def solution(mesh):
    dp, mp = AXES[:3], AXES[3:]
    split = Mesh(mesh.devices.reshape(2, mesh.shape["dp"] // 4, 2, Z, 2), AXES)
    return jax.shard_map(
        shards,
        mesh=split,
        in_specs=(P(AXES, None), P(), P(None, mp), P(mp), P(dp, mp)),
        out_specs=(P(dp, mp), P(AXES, None), P(dp), P(AXES)),
        check_vma=False,
    )
```

time: 454 us -> 127 us (0.28)
  waiting for transfers between devices: 357 us -> 0 us
  Pallas kernels: 0 us -> 116 us
  blocking collectives: 41.2 us -> 0 us
  matrix products: 29.8 us -> 0 us
  between operations: 13.9 us -> 0.64 us
  other arithmetic: 7.41 us -> 1.29 us
    reduce_scatter x2 -> x0, waiting for transfers between devices: 214 us -> none  [summed_rows(): total = lax.psum_scatter(total, axis, scatter_dimension=0, tiled=True)]
    all_gather x1 -> x0, waiting for transfers between devices: 142 us -> none  [shards(): project_normed = lax.all_gather(normed, MP, axis=0, tiled=True)]
    pallas_call x0 -> x1, Pallas kernels: none -> 116 us  [shards(): pl.pallas_call(kernel, name='qkv_ring', out_shape=(jax.ShapeDtypeStruct((...]
    psum x2 -> x0, blocking collectives: 41.2 us -> none  [over_axes(): value = lax.psum(value, axis)]
    dot_general x2 -> x0, matrix products: 29.8 us -> none  [the longest x1 15.7 us: shards(): jnp.dot(project_normed, qkv_weight, preferred_element_type=jnp.float32)]
    unnamed x10 -> x3, local copies, waits for them, and re-layouts: 0.69 us -> 5.61 us
  transfers between devices with their start and end apart: 3 -> 0, of which waited for: 3 -> 0; matrix products, arithmetic and copies ran while one was open for 0% -> 0% of each run, Pallas kernels for 0% -> 0%
where the time goes in v1:
time: 127 us; the launch traced here: 125 us
  Pallas kernels  116 us (91%)
  local copies, waits for them, and re-layouts  6.88 us (5%)
  other arithmetic  1.29 us (1%)
    pallas_call x1, Pallas kernels, shards(): pl.pallas_call(kernel, name='qkv_ring', out_shape=(jax.ShapeDtypeStruct((...  116 us
    unnamed x3, local copies, waits for them, and re-layouts  5.61 us

profile of v1, /device:TPU:4, one launch (start us, length us, event | category | flops | bytes accessed | tf_op | source)
XLA Modules:
  0.0 125.1 jit_solution(605886822635275192)
XLA Ops:
  0.6 1.3 %reshape.28.bias_h = f32[1,640]{1,0:T(1,128)} reshape(f32[640]{0:T(1024)} %param.10) | data formatting | bytes 5120 | tf_op jit(solution)/shard_map/reshape | solution.py:517
  1.9 116.3 %qkv_ring.1 = (bf16[8,2,32,640]{3,2,1,0:T(8,128)(2,1)}, f32[32,8192]{1,0:T(8,128)}, f32[8,1,1024]{2,1,0:T(1,128)}, f32[1,640]{1,0:T(1,128)}) custom-call(bf16[32,8192]{1,0:T(8,128)(2,1)} %tok_h.1, bf16[8192,640]{1,0:T(8,128)(2,1)} %w_h.1, bf16[8,2,32,640]{3,2,1,0:T(8,128)(2,1)} %bitcast.5, f32[1,8192]{1,0:T(1,128)} %bitcast.7, f32[1,640]{1,0:T(1,128)} %reshape.28.bias_h, ...), custom_call_target="tpu_custom_call" | custom-call | tf_op jit(solution)/shard_map/qkv_ring/pallas_call | solution.py:461
  118.2 1.3 %reduce = f32[640]{0:T(1024)} reduce(f32[1,640]{1,0:T(1,128)} %get-tuple-element.11, f32[]{:T(128)} %constant.7), dimensions={0}, to_apply=%get-tuple-element.11.reduce_sub_computation | reduce | bytes 5124 | tf_op jit(solution)/shard_map/qkv_ring/pallas_call | solution.py:461
  119.5 2.0 %copy.14 = bf16[512,640]{1,0:T(8,128)(2,1)} copy(bf16[512,640]{1,0:T(8,128)(2,1)} %bitcast.4) | data formatting | bytes 1310720
  121.4 2.3 %copy.15 = f32[32,8192]{1,0:T(8,128)} copy(f32[32,8192]{1,0:T(8,128)} %get-tuple-element.17) | data formatting | bytes 2097152
  123.7 1.4 %copy.16 = f32[8192]{0:T(1024)} copy(f32[8192]{0:T(1024)} %bitcast.6) | data formatting | bytes 65536

commit v2 on v1

--- a/solution.py
+++ b/solution.py
@@ -30,8 +30,8 @@
     tok_h, w_h, qg_h, gain_h, bias_h, cos_h, sin_h,
     qkv_o, tg_o, gg_o, bg_o,
     w, tok, nrm, part, rb, sb, qb, qp, jl, out, ng, scl, inner, acc,
-    gp, gr, gs, gy, gf, gain, bias, bgv, cosv, sinv,
-    ag_r, ag_s, w_r, w_s, d_r, d_s, rs_r, rs_s, q_r, q_s, b_r, b_s, o_r, o_s,
+    gp, gr, gs, gy, gf, gain, bias, b_own, b_far, bgv, bg1, cosv, sinv,
+    ag_r, ag_s, w_r, w_s, x_r, x_s, d_r, d_s, rs_r, rs_s, q_r, q_s, b_r, b_s, o_r, o_s,
     g_r, g_s, gy_r, gy_s, gf_r, gf_s, loc,
 ):
     rows, dim = tok_h.shape
@@ -39,7 +39,7 @@
     F = dim // N
     H = F // 2
     half = dim // 2
-    yh, core, z, yl = (lax.axis_index(a) for a in ("yh", "core", "z", "yl"))
+    yh, x, core, z, yl = (lax.axis_index(a) for a in AXES)
 
     def zz(k):
         return lax.rem(z + (k + Z), Z)
@@ -47,6 +47,9 @@
     direct = {"yl": 1 - yl}
     other = {"yh": 1 - yh, "yl": 1 - yl}
     sibling = {"core": 1 - core}
+    nx = lax.axis_size("x")
+    beside = [{"x": lax.rem(x + 1, nx)}, {"x": lax.rem(x + nx - 1, nx)}]
+    side = lax.rem(x, 2)
     own = pl.ds(pl.multiple_of(yl * width, 128), width)
     far = pl.ds(pl.multiple_of((1 - yl) * width, 128), width)
 
@@ -56,7 +59,7 @@
         pltpu.make_async_copy(cos_h, cosv, loc.at[2]),
         pltpu.make_async_copy(sin_h, sinv, loc.at[3]),
         pltpu.make_async_copy(gain_h, gain, loc.at[4]),
-        pltpu.make_async_copy(bias_h, bias.at[:, own], loc.at[5]),
+        pltpu.make_async_copy(bias_h, b_own, loc.at[5]),
         pltpu.make_async_copy(w_h, w.at[:, own], loc.at[6]),
     ]
     for copy in local:
@@ -65,9 +68,9 @@
     barrier = pltpu.get_barrier_semaphore()
     for k in range(1, Z):
         pl.semaphore_signal(barrier, inc=1, device_id={"z": zz(k)}, device_id_type=MESH)
-    for where in (direct, other, sibling):
+    for where in (direct, other, sibling, *beside):
         pl.semaphore_signal(barrier, inc=1, device_id=where, device_id_type=MESH)
-    pl.semaphore_wait(barrier, Z + 2)
+    pl.semaphore_wait(barrier, Z + 4)
 
     def ag_half(d, k):
         return d if k % 2 == 0 else 1 - d
@@ -85,32 +88,48 @@
 
     q_copy = rcopy(qg_h.at[:, 1 - yl], qp, q_s.at[0], q_r.at[0], **direct)
     q_copy.start()
-    b_copy = rcopy(bias_h, bias.at[:, own], b_s.at[0], b_r.at[0], **direct)
+    b_copy = rcopy(bias_h, b_far, b_s.at[0], b_r.at[0], **direct)
     b_copy.start()
 
-    share = F // 2
-    piece = share // 2
+    piece = F // 8
+
+    def w_rows(j, par, who, s, n):
+        return pl.ds(pl.multiple_of(j * F + par * 4 * piece + who * 2 * piece + s * piece, piece), n * piece)
 
     def w_copy(j, s):
-        at = pl.ds(pl.multiple_of(j * F + core * share + s * piece, piece), piece)
+        at = w_rows(j, side, core, s, 1)
         return rcopy(w_h.at[at], w.at[at, own], w_s.at[s, j], w_r.at[s, j], **(direct if s == 0 else other))
 
     def w_got(j, s):
-        at = pl.ds(pl.multiple_of(j * F + core * share + s * piece, piece), piece)
-        return rcopy(w.at[at, far], w.at[at, far], w_s.at[s, j], w_r.at[s, j], **(direct if s == 0 else other))
-
-    def d_copy(j):
-        at = pl.ds(pl.multiple_of(j * F + core * share, share), share)
-        return rcopy(w.at[at, far], w.at[at, far], d_s.at[j], d_r.at[j], **sibling)
-
-    def d_got(j):
-        at = pl.ds(pl.multiple_of(j * F + (1 - core) * share, share), share)
-        return rcopy(w.at[at, far], w.at[at, far], d_s.at[j], d_r.at[j], **sibling)
+        spot = w.at[w_rows(j, side, core, s, 1), far]
+        return rcopy(spot, spot, w_s.at[s, j], w_r.at[s, j], **(direct if s == 0 else other))
+
+    def x_copy(j, s):
+        spot = w.at[w_rows(j, side, core, s, 1), far]
+        return rcopy(spot, spot, x_s.at[s, j], x_r.at[s, j], **beside[s])
+
+    def x_got(j, s):
+        spot = w.at[w_rows(j, 1 - side, core, s, 1), far]
+        return rcopy(spot, spot, x_s.at[s, j], x_r.at[s, j], **beside[1 - s])
+
+    def d_copy(j, k):
+        spot = w.at[w_rows(j, side if k == 0 else 1 - side, core, 0, 2), far]
+        return rcopy(spot, spot, d_s.at[k, j], d_r.at[k, j], **sibling)
+
+    def d_got(j, k):
+        spot = w.at[w_rows(j, side if k == 0 else 1 - side, 1 - core, 0, 2), far]
+        return rcopy(spot, spot, d_s.at[k, j], d_r.at[k, j], **sibling)
 
     def hand_on(j):
-        w_got(j, 0).wait_recv()
-        w_got(j, 1).wait_recv()
-        d_copy(j).start()
+        for s in range(2):
+            w_got(j, s).wait_recv()
+            x_copy(j, s).start()
+        d_copy(j, 0).start()
+
+    def hand_over(j):
+        for s in range(2):
+            x_got(j, s).wait_recv()
+        d_copy(j, 1).start()
 
     for j in range(N):
         w_copy(j, 0).start()
@@ -176,50 +195,24 @@
 
         lax.fori_loop(0, Z, one, 0)
 
-    for k in range(1, 5):
-        local[k].wait()
-    own_columns()
-    local[0].wait()
-    norm_block(z)
-    local[5].wait()
-    bg_copy = pltpu.make_async_copy(bgv, bg_o, loc.at[7])
-    bg_copy.start()
-
-    for k in range(PER):
-        for d in range(2):
-            block = zz(-1 - k // 2) if d == 0 else zz(1 + k // 2)
-            cols = pl.ds(ag_half(d, k) * half, half)
-            spot = tok.at[block, :, cols]
-            rcopy(spot, spot, ag_s.at[d, k], ag_r.at[d, k], z=z).wait_recv()
-            if k + 2 < PER:
-                ag_copy(d, k + 2).start()
-        if k == 1:
-            q_copy.wait_recv()
-            b_copy.wait_recv()
-            far_columns()
-        if k % 2 == 1:
-            norm_block(zz(-1 - k // 2))
-            norm_block(zz(1 + k // 2))
-        if k == 6:
-            norm_block(zz(4))
-        if 4 <= k:
-            hand_on(k - 4)
-    local[6].wait()
-
     bt = min(256, F)
 
-    def backward_chunk(c):
-        @pl.when(c < 6)
-        def _():
-            d_got(c).wait_recv()
-
+    def backward_part(c, first, count):
         def one(t, carry):
             at = pl.ds(pl.multiple_of(c * F + t * bt, bt), bt)
             got = lax.dot_general(jl[...], w[at, :], (((1,), (1,)), ((), ())), preferred_element_type=f32)
             part[:, :, at] = got.reshape(Z, rows, bt)
             return carry
 
-        lax.fori_loop(0, F // bt, one, 0)
+        lax.fori_loop(first, first + count, one, 0)
+
+    def weights_here(c):
+        d_got(c, 0).wait_recv()
+        d_got(c, 1).wait_recv()
+
+    def backward_chunk(c):
+        weights_here(c)
+        backward_part(c, 0, F // bt)
 
     def span(c, hf):
         return pl.ds(pl.multiple_of(c * F + hf * H, H), H)
@@ -236,17 +229,22 @@
                 rs_copy(d, c, 4 * short, sb.at[d, c, short]).start()
 
     def later_hop(c, hop):
-        for d in range(2):
-            for short in range(2):
-                if short and hop == 4:
-                    continue
-                hf = d if short == 0 else 1 - d
-                dist = 5 - hop - short
-                slot = 4 * short + hop - 2
-                rs_copy(d, c, slot, rb.at[d, c, slot]).wait_recv()
-                mine = part[zz(dist if d == 0 else -dist), :, span(c, hf)]
-                rb[d, c, slot] = (rb[d, c, slot].astype(f32) + mine).astype(bf16)
-                rs_copy(d, c, slot + 1, rb.at[d, c, slot]).start()
+        def one(d, short):
+            hf = d if short == 0 else 1 - d
+            dist = 4 - hop - short
+            slot = 4 * short + hop - 1
+            rs_copy(d, c, slot, rb.at[d, c, slot]).wait_recv()
+            mine = part[zz(dist if d == 0 else -dist), :, span(c, hf)]
+            rb[d, c, slot] = (rb[d, c, slot].astype(f32) + mine).astype(bf16)
+            rs_copy(d, c, slot + 1, rb.at[d, c, slot]).start()
+
+        one(0, 0)
+        one(1, 0)
+
+        @pl.when(hop < 3)
+        def _():
+            one(0, 1)
+            one(1, 1)
 
     def finish(c):
         for d in range(2):
@@ -281,19 +279,18 @@
 
     gy_copy = rcopy(gs, gy, gy_s.at[0], gy_r.at[0], **direct)
 
-    def forward_tile(t):
-        n = jnp.where(yl == 0, t, 4 - t)
+    def forward_quarter(t, k):
+        n = jnp.where(yl == 0, 4 - t, t)
         cols = pl.ds(pl.multiple_of(n * 256, 256), 256)
         deep = dim // 4
-        acc[...] = jnp.broadcast_to(bias[:, cols], acc.shape)
-
-        def one(k, carry):
-            at = pl.ds(pl.multiple_of(k * deep, deep), deep)
-            lhs = nrm[:, :, at].reshape(Z * rows, deep)
-            acc[...] += jnp.dot(lhs, w[at, cols], preferred_element_type=f32)
-            return carry
-
-        lax.fori_loop(0, 4, one, 0)
+
+        @pl.when(k == 0)
+        def _():
+            acc[...] = jnp.broadcast_to(bias[:, cols], acc.shape)
+
+        at = pl.ds(pl.multiple_of(k * deep, deep), deep)
+        lhs = nrm[:, :, at].reshape(Z * rows, deep)
+        acc[...] += jnp.dot(lhs, w[at, cols], preferred_element_type=f32)
 
         def spin(b, carry):
             at = pl.ds(pl.multiple_of(b * rows, rows), rows)
@@ -305,76 +302,130 @@
                 out[b, :, pl.ds(pl.multiple_of(n * 256 + h * HEAD, HEAD), HEAD)] = r.astype(bf16)
             return carry
 
-        lax.fori_loop(0, Z, spin, 0)
+        @pl.when(k == 3)
+        def _():
+            lax.fori_loop(0, Z, spin, 0)
 
     o_copy = rcopy(out.at[:, :, far], qkv_o.at[:, yl], o_s.at[0], o_r.at[0], **direct)
     o_local = pltpu.make_async_copy(out.at[:, :, own], qkv_o.at[:, yl], loc.at[8])
 
     inner[...] = jnp.zeros_like(inner)
 
-    def iteration(i, carry):
-        @pl.when(i < N)
-        def _():
-            backward_chunk(i)
-            first_hop(i)
-
-        for hop in (2, 3, 4):
-            @pl.when((i >= hop - 1) & (i < N + hop - 1))
-            def _(hop=hop):
-                later_hop(i - hop + 1, hop)
-
-        @pl.when(i >= 4)
-        def _():
-            finish(i - 4)
-
-        @pl.when(i < N)
-        def _():
-            gain_part(i)
-
-            @pl.when(i != z)
+    for k in range(1, 5):
+        local[k].wait()
+    own_columns()
+    local[0].wait()
+    norm_block(z)
+    local[5].wait()
+    bg1[...] = bgv[...].reshape(width)
+    bg_copy = pltpu.make_async_copy(bg1, bg_o, loc.at[7])
+    bg_copy.start()
+
+    for k in range(PER):
+        for d in range(2):
+            block = zz(-1 - k // 2) if d == 0 else zz(1 + k // 2)
+            cols = pl.ds(ag_half(d, k) * half, half)
+            spot = tok.at[block, :, cols]
+            rcopy(spot, spot, ag_s.at[d, k], ag_r.at[d, k], z=zz(1)).wait_recv()
+            if k + 2 < PER:
+                ag_copy(d, k + 2).start()
+        for j in {1: (0,), 2: (1, 2), 3: (3, 4), 4: (5,), 5: (6, 7)}.get(k, ()):
+            hand_on(j)
+        for j in {3: (0,), 4: (1, 2), 5: (3, 4), 6: (5,)}.get(k, ()):
+            hand_over(j)
+        if k == 1:
+            q_copy.wait_recv()
+            b_copy.wait_recv()
+            bias[:, own] = b_own[...].reshape(1, width)
+            bias[:, far] = b_far[...].reshape(1, width)
+            far_columns()
+        if k in (1, 3):
+            norm_block(zz(-1 - k // 2))
+            norm_block(zz(1 + k // 2))
+        if k == 4:
+            local[6].wait()
+            backward_chunk(0)
+        if k == 5:
+            first_hop(0)
+            backward_chunk(1)
+            first_hop(1)
+            norm_block(zz(-3))
+            norm_block(zz(3))
+            backward_chunk(2)
+            first_hop(2)
+        if k == 6:
+            backward_chunk(3)
+            first_hop(3)
+            norm_block(zz(4))
+
+    def event(e, carry):
+        r = lax.rem(e, 16)
+        hop = r // 4
+        c = e // 16 * 4 + lax.rem(r, 4)
+
+        @pl.when((hop == 0) & (e < 32))
+        def _():
+            first_hop(c)
+
+        @pl.when((hop > 0) & (e < 32))
+        def _():
+            later_hop(c, hop)
+
+        @pl.when((e == 4) | (e == 6))
+        def _():
+            hand_over(6 + (e - 4) // 2)
+
+        @pl.when(e < 12)
+        def _():
+            c = 4 + (e - 4) // 2
+            odd = lax.rem(e, 2)
+
+            @pl.when(odd == 0)
             def _():
-                g_send(i).start()
-
-        @pl.when(i == z + 1)
+                weights_here(c)
+            backward_part(c, odd * (F // bt // 2), F // bt // 2)
+
+        @pl.when((e < 8) | ((e >= 12) & (e < 16)))
+        def _():
+            c = jnp.where(e < 8, e - 4, e - 8)
+            gain_part(c)
+
+            @pl.when(c != z)
+            def _():
+                g_send(c).start()
+
+        @pl.when((e >= 12) & (e < 32))
+        def _():
+            forward_quarter((e - 12) // 4, lax.rem(e, 4))
+
+        @pl.when(e == 21)
         def _():
             total = gp[z]
             for k in range(1, Z):
                 spot = gr.at[zz(k)]
-                rcopy(spot, spot, g_s.at[zz(k)], g_r.at[zz(k)], z=z).wait_recv()
+                rcopy(spot, spot, g_s.at[zz(k)], g_r.at[zz(k)], z=zz(1)).wait_recv()
                 total = total + gr[zz(k)]
             gs[...] = total
             gy_copy.start()
 
-        @pl.when(i == z + 2)
+        @pl.when(e == 24)
+        def _():
+            o_copy.start()
+
+        @pl.when(e == 25)
         def _():
             gy_copy.wait_recv()
             gf[z] = gs[...] + gy[...]
             for k in range(1, Z):
                 gf_send(k).start()
 
-        @pl.when(i < 3)
-        def _():
-            hand_on(i + 3)
-
-        @pl.when((i == 4) | (i == 5))
-        def _():
-            hand_on(i + 2)
-
-        @pl.when((i < 2) | ((i >= 5) & (i < 8)))
-        def _():
-            @pl.when(i == 5)
-            def _():
-                d_got(6).wait_recv()
-                d_got(7).wait_recv()
-            forward_tile(jnp.where(i < 2, i, i - 3))
-
-        @pl.when(i == 7)
-        def _():
-            o_copy.start()
-            o_local.start()
+        @pl.when(((e >= 24) & (e < 28)) | (e >= 32))
+        def _():
+            finish(jnp.where(e < 28, e - 24, e - 28))
         return carry
 
-    lax.fori_loop(0, N + 4, iteration, 0)
+    lax.fori_loop(4, 36, event, 0)
+    o_local.start()
 
     mean = jnp.sum(inner[...], axis=1, keepdims=True) / dim
     s = scl[z]
@@ -398,7 +449,7 @@
 
     for k in range(1, Z):
         spot = gf.at[zz(k)]
-        rcopy(spot, spot, gf_s.at[k], gf_r.at[zz(k)], z=z).wait_recv()
+        rcopy(spot, spot, gf_s.at[k], gf_r.at[zz(k)], z=zz(1)).wait_recv()
     g_out = pltpu.make_async_copy(gf, gg_o, loc.at[13])
     g_out.start()
 
@@ -412,7 +463,9 @@
     def sent(c, carry):
         w_copy(c, 0).wait_send()
         w_copy(c, 1).wait_send()
-        d_copy(c).wait_send()
+        for k in range(2):
+            x_copy(c, k).wait_send()
+            d_copy(c, k).wait_send()
         for d in range(2):
             for slot in range(PER):
                 rs_copy(d, c, slot, rb.at[d, c, slot]).wait_send()
@@ -465,7 +518,7 @@
             jax.ShapeDtypeStruct((Z, 2, rows, width), bf16),
             jax.ShapeDtypeStruct((rows, dim), f32),
             jax.ShapeDtypeStruct((Z, 1, F), f32),
-            jax.ShapeDtypeStruct((1, width), f32),
+            jax.ShapeDtypeStruct((width,), f32),
         ),
         in_specs=[any_spec] * 7,
         out_specs=(any_spec,) * 4,
@@ -491,12 +544,16 @@
             V((Z, 1, F), f32),
             V((1, dim), f32),
             V((1, both), f32),
+            V((width,), f32),
+            V((width,), f32),
             V((1, width), f32),
+            V((width,), f32),
             V(cos.shape, f32),
             V(sin.shape, f32),
             dma((2, PER)), dma((2, PER)),
             dma((2, N)), dma((2, N)),
-            dma((N,)), dma((N,)),
+            dma((2, N)), dma((2, N)),
+            dma((2, N)), dma((2, N)),
             dma((2, N, PER)), dma((2, N, PER)),
             dma((1,)), dma((1,)),
             dma((1,)), dma((1,)),
@@ -514,7 +571,7 @@
         qkv_weight,
         qkv_grad.reshape(Z, 2, rows, width),
         norm_gain.reshape(1, dim),
-        qkv_bias.reshape(1, width),
+        qkv_bias,
         jnp.asarray(cos),
         jnp.asarray(sin),
     )
@@ -522,7 +579,7 @@
         qkv.reshape(2 * Z * rows, width),
         tokens_grad,
         gain_grad.reshape(dim),
-        bias_grad.reshape(width),
+        bias_grad,
     )
 
 

time: 127 us -> 104 us (0.82); the launches traced: 125 us -> 104 us
  Pallas kernels: 116 us -> 96.4 us
  other arithmetic: 1.29 us -> 0 us
    pallas_call x1, Pallas kernels: 116 us -> 96.4 us  [shards(): pl.pallas_call(kernel, name='qkv_ring', out_shape=(jax.ShapeDtypeStruct((...]
    pallas_call x1 -> x0, other arithmetic: 1.29 us -> none  [shards(): pl.pallas_call(kernel, name='qkv_ring', out_shape=(jax.ShapeDtypeStruct((...]
    unnamed x3 -> x4, local copies, waits for them, and re-layouts: 5.61 us -> 6.88 us
where the time goes in v2:
time: 104 us
  Pallas kernels  96.4 us (93%)
  local copies, waits for them, and re-layouts  6.88 us (7%)
    pallas_call x1, Pallas kernels, shards(): pl.pallas_call(kernel, name='qkv_ring', out_shape=(jax.ShapeDtypeStruct((...  96.4 us
    unnamed x4, local copies, waits for them, and re-layouts  6.88 us

profile of v2, /device:TPU:4, one launch (start us, length us, event | category | flops | bytes accessed | tf_op | source)
XLA Modules:
  0.0 104.0 jit_solution(3461727925815792273)
XLA Ops:
  0.6 96.4 %qkv_ring.1 = (bf16[8,2,32,640]{3,2,1,0:T(8,128)(2,1)}, f32[32,8192]{1,0:T(8,128)}, f32[8,1,1024]{2,1,0:T(1,128)}, f32[640]{0:T(1024)}) custom-call(bf16[32,8192]{1,0:T(8,128)(2,1)} %tok_h.1, bf16[8192,640]{1,0:T(8,128)(2,1)} %w_h.1, bf16[8,2,32,640]{3,2,1,0:T(8,128)(2,1)} %bitcast.4, f32[1,8192]{1,0:T(1,128)} %bitcast.6, f32[640]{0:T(1024)} %bias_h.1, ...), custom_call_target="tpu_custom_call" | custom-call | tf_op jit(solution)/shard_map/qkv_ring/pallas_call | solution.py:514
  97.1 2.0 %copy.15 = bf16[512,640]{1,0:T(8,128)(2,1)} copy(bf16[512,640]{1,0:T(8,128)(2,1)} %bitcast.5) | data formatting | bytes 1310720
  99.1 2.3 %copy.16 = f32[32,8192]{1,0:T(8,128)} copy(f32[32,8192]{1,0:T(8,128)} %get-tuple-element.17) | data formatting | bytes 2097152
  101.3 1.4 %copy.17 = f32[8192]{0:T(1024)} copy(f32[8192]{0:T(1024)} %bitcast.7) | data formatting | bytes 65536
  102.7 1.3 %copy.18 = f32[640]{0:T(1024)} copy(f32[640]{0:T(1024)} %get-tuple-element.19) | data formatting | bytes 5120

commit v3 on v2

--- a/solution.py
+++ b/solution.py
@@ -28,11 +28,11 @@
 
 def kernel(
     tok_h, w_h, qg_h, gain_h, bias_h, cos_h, sin_h,
-    qkv_o, tg_o, gg_o, bg_o,
-    w, tok, nrm, part, rb, sb, qb, qp, jl, out, ng, scl, inner, acc,
+    qkv_o, ng_o, st_o, gg_o, bg_o,
+    w, tok, nrm, part, rb, sb, qb, qp, jl, out, ng, st, scl, inner, acc,
     gp, gr, gs, gy, gf, gain, bias, b_own, b_far, bgv, bg1, cosv, sinv,
     ag_r, ag_s, w_r, w_s, x_r, x_s, d_r, d_s, rs_r, rs_s, q_r, q_s, b_r, b_s, o_r, o_s,
-    g_r, g_s, gy_r, gy_s, gf_r, gf_s, loc,
+    g_r, g_s, gy_r, gy_s, gf_r, gf_s, ng_s, loc,
 ):
     rows, dim = tok_h.shape
     width = w_h.shape[1]
@@ -66,11 +66,10 @@
         copy.start()
 
     barrier = pltpu.get_barrier_semaphore()
-    for k in range(1, Z):
-        pl.semaphore_signal(barrier, inc=1, device_id={"z": zz(k)}, device_id_type=MESH)
-    for where in (direct, other, sibling, *beside):
+    for where in ({"z": zz(1)}, {"z": zz(-1)}, direct, other, sibling, *beside):
         pl.semaphore_signal(barrier, inc=1, device_id=where, device_id_type=MESH)
-    pl.semaphore_wait(barrier, Z + 4)
+    pl.semaphore_wait(barrier, 7)
+    local[0].wait()
 
     def ag_half(d, k):
         return d if k % 2 == 0 else 1 - d
@@ -79,8 +78,8 @@
         step = k // 2
         block = zz(-step) if d == 0 else zz(step)
         cols = pl.ds(ag_half(d, k) * half, half)
-        src = tok_h.at[:, cols] if step == 0 else tok.at[block, :, cols]
-        return rcopy(src, tok.at[block, :, cols], ag_s.at[d, k], ag_r.at[d, k], z=zz(1 if d == 0 else -1))
+        spot = tok.at[block, :, cols]
+        return rcopy(spot, spot, ag_s.at[d, k], ag_r.at[d, k], z=zz(1 if d == 0 else -1))
 
     for k in range(2):
         for d in range(2):
@@ -245,6 +244,10 @@
         def _():
             one(0, 1)
             one(1, 1)
+
+    def ng_copy(c):
+        at = pl.ds(pl.multiple_of(c * F, F), F)
+        return pltpu.make_async_copy(ng.at[:, at], ng_o.at[:, at], ng_s.at[c])
 
     def finish(c):
         for d in range(2):
@@ -259,6 +262,7 @@
             for q in range(H // 128):
                 total = total + t[:, q * 128:(q + 1) * 128]
         inner[...] = total
+        ng_copy(c).start()
 
     def gain_part(c):
         def one(t, carry):
@@ -309,12 +313,12 @@
     o_copy = rcopy(out.at[:, :, far], qkv_o.at[:, yl], o_s.at[0], o_r.at[0], **direct)
     o_local = pltpu.make_async_copy(out.at[:, :, own], qkv_o.at[:, yl], loc.at[8])
 
+    g_out = pltpu.make_async_copy(gf, gg_o, loc.at[10])
     inner[...] = jnp.zeros_like(inner)
 
     for k in range(1, 5):
         local[k].wait()
     own_columns()
-    local[0].wait()
     norm_block(z)
     local[5].wait()
     bg1[...] = bgv[...].reshape(width)
@@ -371,9 +375,9 @@
         def _():
             later_hop(c, hop)
 
-        @pl.when((e == 4) | (e == 6))
-        def _():
-            hand_over(6 + (e - 4) // 2)
+        @pl.when((e == 5) | (e == 7))
+        def _():
+            hand_over(6 + (e - 5) // 2)
 
         @pl.when(e < 12)
         def _():
@@ -385,9 +389,9 @@
                 weights_here(c)
             backward_part(c, odd * (F // bt // 2), F // bt // 2)
 
-        @pl.when((e < 8) | ((e >= 12) & (e < 16)))
-        def _():
-            c = jnp.where(e < 8, e - 4, e - 8)
+        @pl.when((e >= 8) & (e < 16))
+        def _():
+            c = e - 8
             gain_part(c)
 
             @pl.when(c != z)
@@ -419,70 +423,125 @@
             for k in range(1, Z):
                 gf_send(k).start()
 
+        @pl.when((e >= 24) & (e < 32))
+        def _():
+            c = e - 24
+            for k in range(2):
+                w_copy(c, k).wait_send()
+                x_copy(c, k).wait_send()
+                d_copy(c, k).wait_send()
+
+            @pl.when(c != z)
+            def _():
+                g_send(c).wait_send()
+
+        @pl.when(e >= 28)
+        def _():
+            c = e - 28
+            for d in range(2):
+                for slot in range(PER):
+                    rs_copy(d, c, slot, rb.at[d, c, slot]).wait_send()
+
+        @pl.when(e == 28)
+        def _():
+            for d in range(2):
+                for k in range(PER):
+                    ag_copy(d, k).wait_send()
+            q_copy.wait_send()
+            b_copy.wait_send()
+            gy_copy.wait_send()
+
+        @pl.when(e == 32)
+        def _():
+            o_local.start()
+
+        @pl.when(e == 33)
+        def _():
+            for k in range(1, Z):
+                spot = gf.at[zz(k)]
+                rcopy(spot, spot, gf_s.at[k], gf_r.at[zz(k)], z=zz(1)).wait_recv()
+            g_out.start()
+
         @pl.when(((e >= 24) & (e < 28)) | (e >= 32))
         def _():
             finish(jnp.where(e < 28, e - 24, e - 28))
         return carry
 
     lax.fori_loop(4, 36, event, 0)
-    o_local.start()
-
     mean = jnp.sum(inner[...], axis=1, keepdims=True) / dim
     s = scl[z]
-    k3 = s * s * s * jnp.broadcast_to(mean, s.shape)
-    s4 = jnp.concatenate([s] * 4, axis=1)
-    k4 = jnp.concatenate([k3] * 4, axis=1)
-
-    def last(i, carry):
-        at = pl.ds(pl.multiple_of(i * 512, 512), 512)
-        ng[:, at] = s4 * gain[:, at] * ng[:, at] - tok[z, :, at].astype(f32) * k4
-        return carry
-
-    outs = []
-    for q in range(4):
-        per = dim // 2048
-        lax.fori_loop(q * per, (q + 1) * per, last, 0)
-        at = pl.ds(q * (dim // 4), dim // 4)
-        copy = pltpu.make_async_copy(ng.at[:, at], tg_o.at[:, at], loc.at[9 + q])
-        copy.start()
-        outs.append(copy)
-
-    for k in range(1, Z):
-        spot = gf.at[zz(k)]
-        rcopy(spot, spot, gf_s.at[k], gf_r.at[zz(k)], z=zz(1)).wait_recv()
-    g_out = pltpu.make_async_copy(gf, gg_o, loc.at[13])
-    g_out.start()
-
-    for d in range(2):
-        for k in range(PER):
-            ag_copy(d, k).wait_send()
-    q_copy.wait_send()
-    b_copy.wait_send()
-    gy_copy.wait_send()
-
-    def sent(c, carry):
-        w_copy(c, 0).wait_send()
-        w_copy(c, 1).wait_send()
-        for k in range(2):
-            x_copy(c, k).wait_send()
-            d_copy(c, k).wait_send()
-        for d in range(2):
-            for slot in range(PER):
-                rs_copy(d, c, slot, rb.at[d, c, slot]).wait_send()
-
-        @pl.when(c != z)
-        def _():
-            g_send(c).wait_send()
-        return carry
-
-    lax.fori_loop(0, N, sent, 0)
+    st[0] = s
+    st[1] = s * s * s * jnp.broadcast_to(mean, s.shape)
+    st_copy = pltpu.make_async_copy(st, st_o, loc.at[9])
+    st_copy.start()
     for k in range(1, Z):
         gf_send(k).wait_send()
+    bg_copy.wait()
     o_copy.wait()
     o_local.wait()
-    bg_copy.wait()
     g_out.wait()
-    for copy in outs:
+    for c in range(N):
+        ng_copy(c).wait()
+    st_copy.wait()
+
+
+def settle(
+    qkv_i, ng_i, st_i, gg_i, bg_i, tok_h, gain_h, qkv_o, tg_o, gg_o, bg_o,
+    qkv, ng, st, gg, bg, tok, gain, sem_i, sem_o, ng_s, tg_s,
+):
+    rows, dim = ng.shape
+    parts = ng_s.shape[0]
+    wide = dim // parts
+    half = qkv.shape[0] // 2
+
+    def loads():
+        yield pltpu.make_async_copy(st_i, st, sem_i.at[0])
+        yield pltpu.make_async_copy(gain_h, gain, sem_i.at[1])
+        yield pltpu.make_async_copy(tok_h, tok, sem_i.at[2])
+
+    first = list(loads())
+    for copy in first:
+        copy.start()
+    pieces = []
+    for q in range(parts):
+        at = pl.ds(q * wide, wide)
+        copy = pltpu.make_async_copy(ng_i.at[:, at], ng.at[:, at], ng_s.at[q])
+        copy.start()
+        pieces.append(copy)
+    through = []
+    for k, (src, mid, dst) in enumerate((
+        (qkv_i.at[pl.ds(0, half)], qkv.at[pl.ds(0, half)], qkv_o.at[pl.ds(0, half)]),
+        (qkv_i.at[pl.ds(half, half)], qkv.at[pl.ds(half, half)], qkv_o.at[pl.ds(half, half)]),
+        (gg_i, gg, gg_o),
+        (bg_i, bg, bg_o),
+    )):
+        copy = pltpu.make_async_copy(src, mid, sem_i.at[3 + k])
+        copy.start()
+        through.append((copy, pltpu.make_async_copy(mid, dst, sem_o.at[k])))
+    for copy in first:
+        copy.wait()
+    step = 512
+    s = jnp.concatenate([st[0]] * (step // 128), axis=1)
+    k = jnp.concatenate([st[1]] * (step // 128), axis=1)
+    sent = []
+    for q in range(parts):
+        pieces[q].wait()
+
+        def one(i, carry):
+            at = pl.ds(pl.multiple_of(q * wide + i * step, step), step)
+            ng[:, at] = s * gain[:, at] * ng[:, at] - tok[:, at].astype(f32) * k
+            return carry
+
+        lax.fori_loop(0, wide // step, one, 0)
+        at = pl.ds(q * wide, wide)
+        copy = pltpu.make_async_copy(ng.at[:, at], tg_o.at[:, at], tg_s.at[q])
+        copy.start()
+        sent.append(copy)
+        got, put = through[q]
+        got.wait()
+        put.start()
+        sent.append(put)
+    for copy in sent:
         copy.wait()
 
 
@@ -511,17 +570,18 @@
     any_spec = pl.BlockSpec(memory_space=pl.ANY)
     dma = pltpu.SemaphoreType.DMA
     V = pltpu.VMEM
-    qkv, tokens_grad, gain_grad, bias_grad = pl.pallas_call(
+    raw = pl.pallas_call(
         kernel,
         name="qkv_ring",
         out_shape=(
             jax.ShapeDtypeStruct((Z, 2, rows, width), bf16),
             jax.ShapeDtypeStruct((rows, dim), f32),
+            jax.ShapeDtypeStruct((2, rows, 128), f32),
             jax.ShapeDtypeStruct((Z, 1, F), f32),
             jax.ShapeDtypeStruct((width,), f32),
         ),
         in_specs=[any_spec] * 7,
-        out_specs=(any_spec,) * 4,
+        out_specs=(any_spec,) * 5,
         scratch_shapes=[
             V((dim, both), bf16),
             V((Z, rows, dim), bf16),
@@ -534,6 +594,7 @@
             V((Z * rows, both), bf16),
             V((Z, rows, both), bf16),
             V((rows, dim), f32),
+            V((2, rows, 128), f32),
             V((Z, rows, 128), f32),
             V((rows, 128), f32),
             V((Z * rows, 256), f32),
@@ -561,6 +622,7 @@
             dma((Z,)), dma((Z,)),
             dma((1,)), dma((1,)),
             dma((Z,)), dma((Z,)),
+            dma((N,)),
             dma((14,)),
         ],
         compiler_params=pltpu.CompilerParams(
@@ -575,6 +637,29 @@
         jnp.asarray(cos),
         jnp.asarray(sin),
     )
+    qkv, tokens_grad, gain_grad, bias_grad = pl.pallas_call(
+        settle,
+        name="settle",
+        out_shape=(
+            jax.ShapeDtypeStruct((Z, 2, rows, width), bf16),
+            jax.ShapeDtypeStruct((rows, dim), f32),
+            jax.ShapeDtypeStruct((Z, 1, F), f32),
+            jax.ShapeDtypeStruct((width,), f32),
+        ),
+        in_specs=[any_spec] * 7,
+        out_specs=(any_spec,) * 4,
+        scratch_shapes=[
+            V((Z, 2, rows, width), bf16),
+            V((rows, dim), f32),
+            V((2, rows, 128), f32),
+            V((Z, 1, F), f32),
+            V((width,), f32),
+            V((rows, dim), bf16),
+            V((1, dim), f32),
+            dma((7,)), dma((4,)), dma((4,)), dma((4,)),
+        ],
+        compiler_params=pltpu.CompilerParams(vmem_limit_bytes=66_000_000),
+    )(*raw, tokens, norm_gain.reshape(1, dim))
     return (
         qkv.reshape(2 * Z * rows, width),
         tokens_grad,

time: 104 us -> 99 us (0.952)
  local copies, waits for them, and re-layouts: 6.88 us -> 0 us
  Pallas kernels: 96.4 us -> 98.2 us
    unnamed x4 -> x0, local copies, waits for them, and re-layouts: 6.88 us -> none
    pallas_call x0 -> x1, Pallas kernels: none -> 2.57 us  [shards(): pl.pallas_call(settle, name='settle', out_shape=(jax.ShapeDtypeStruct((Z,...]
where the time goes in v3:
time: 99 us; the launch traced here: 98.9 us
  Pallas kernels  98.2 us (99%)
    pallas_call x1, Pallas kernels, shards(): pl.pallas_call(kernel, name='qkv_ring', out_shape=(jax.ShapeDtypeStruct((...  95.7 us
    pallas_call x1, Pallas kernels, shards(): pl.pallas_call(settle, name='settle', out_shape=(jax.ShapeDtypeStruct((Z,...  2.57 us

profile of v3, /device:TPU:4, one launch (start us, length us, event | category | flops | bytes accessed | tf_op | source)
XLA Modules:
  0.0 98.9 jit_solution(17212308849473062246)
XLA Ops:
  0.6 95.7 %qkv_ring.1 = (bf16[8,2,32,640]{3,2,1,0:T(8,128)(2,1)}, f32[32,8192]{1,0:T(8,128)}, f32[2,32,128]{2,1,0:T(8,128)}, f32[8,1,1024]{2,1,0:T(1,128)}, f32[640]{0:T(1024)}) custom-call(bf16[32,8192]{1,0:T(8,128)(2,1)} %tok_h.3, bf16[8192,640]{1,0:T(8,128)(2,1)} %w_h.1, bf16[8,2,32,640]{3,2,1,0:T(8,128)(2,1)} %bitcast.4, f32[1,8192]{1,0:T(1,128)} %bitcast.5, ...), custom_call_target="tpu_custom_call" | custom-call | tf_op jit(solution)/shard_map/qkv_ring/pallas_call | solution.py:573
  96.3 2.6 %settle.1 = (bf16[8,2,32,640]{3,2,1,0:T(8,128)(2,1)}, f32[32,8192]{1,0:T(8,128)}, f32[8,1,1024]{2,1,0:T(1,128)}, f32[640]{0:T(1024)}) custom-call(bf16[8,2,32,640]{3,2,1,0:T(8,128)(2,1)} %get-tuple-element.13.qkv_i, f32[32,8192]{1,0:T(8,128)} %get-tuple-element.14.ng_i, f32[2,32,128]{2,1,0:T(8,128)} %get-tuple-element.15.st_i, ...), custom_call_target="tpu_custom_call" | custom-call | tf_op jit(solution)/shard_map/settle/pallas_call | solution.py:640

commit v4 on v3

--- a/solution.py
+++ b/solution.py
@@ -30,9 +30,9 @@
     tok_h, w_h, qg_h, gain_h, bias_h, cos_h, sin_h,
     qkv_o, ng_o, st_o, gg_o, bg_o,
     w, tok, nrm, part, rb, sb, qb, qp, jl, out, ng, st, scl, inner, acc,
-    gp, gr, gs, gy, gf, gain, bias, b_own, b_far, bgv, bg1, cosv, sinv,
-    ag_r, ag_s, w_r, w_s, x_r, x_s, d_r, d_s, rs_r, rs_s, q_r, q_s, b_r, b_s, o_r, o_s,
-    g_r, g_s, gy_r, gy_s, gf_r, gf_s, ng_s, loc,
+    gp, gr, gy, gf, gain, bias, b_own, b_far, bgv, bg1, cosv, sinv,
+    ag_r, ag_s, w_r, w_s, x_r, d_r, rs_r, rs_s, q_r, q_s, b_r, b_s, o_r, o_s,
+    g_r, g_s, gy_r, gy_s, gf_r, gf_s, gl_r, gl_s, ng_s, loc,
 ):
     rows, dim = tok_h.shape
     width = w_h.shape[1]
@@ -79,7 +79,7 @@
         block = zz(-step) if d == 0 else zz(step)
         cols = pl.ds(ag_half(d, k) * half, half)
         spot = tok.at[block, :, cols]
-        return rcopy(spot, spot, ag_s.at[d, k], ag_r.at[d, k], z=zz(1 if d == 0 else -1))
+        return rcopy(spot, spot, ag_s.at[0], ag_r.at[k], z=zz(1 if d == 0 else -1))
 
     for k in range(2):
         for d in range(2):
@@ -97,37 +97,32 @@
 
     def w_copy(j, s):
         at = w_rows(j, side, core, s, 1)
-        return rcopy(w_h.at[at], w.at[at, own], w_s.at[s, j], w_r.at[s, j], **(direct if s == 0 else other))
-
-    def w_got(j, s):
-        spot = w.at[w_rows(j, side, core, s, 1), far]
-        return rcopy(spot, spot, w_s.at[s, j], w_r.at[s, j], **(direct if s == 0 else other))
+        return rcopy(w_h.at[at], w.at[at, own], w_s.at[0], w_r.at[j], **(direct if s == 0 else other))
+
+    def w_got(j):
+        spot = w.at[w_rows(j, side, core, 0, 2), far]
+        return rcopy(spot, spot, w_s.at[0], w_r.at[j], **direct)
 
     def x_copy(j, s):
         spot = w.at[w_rows(j, side, core, s, 1), far]
-        return rcopy(spot, spot, x_s.at[s, j], x_r.at[s, j], **beside[s])
-
-    def x_got(j, s):
-        spot = w.at[w_rows(j, 1 - side, core, s, 1), far]
-        return rcopy(spot, spot, x_s.at[s, j], x_r.at[s, j], **beside[1 - s])
+        return rcopy(spot, spot, w_s.at[0], x_r.at[j], **beside[s])
+
+    def x_got(j):
+        spot = w.at[w_rows(j, 1 - side, core, 0, 2), far]
+        return rcopy(spot, spot, w_s.at[0], x_r.at[j], **beside[0])
 
     def d_copy(j, k):
         spot = w.at[w_rows(j, side if k == 0 else 1 - side, core, 0, 2), far]
-        return rcopy(spot, spot, d_s.at[k, j], d_r.at[k, j], **sibling)
-
-    def d_got(j, k):
-        spot = w.at[w_rows(j, side if k == 0 else 1 - side, 1 - core, 0, 2), far]
-        return rcopy(spot, spot, d_s.at[k, j], d_r.at[k, j], **sibling)
+        return rcopy(spot, spot, w_s.at[0], d_r.at[j], **sibling)
 
     def hand_on(j):
+        w_got(j).wait_recv()
         for s in range(2):
-            w_got(j, s).wait_recv()
             x_copy(j, s).start()
         d_copy(j, 0).start()
 
     def hand_over(j):
-        for s in range(2):
-            x_got(j, s).wait_recv()
+        x_got(j).wait_recv()
         d_copy(j, 1).start()
 
     for j in range(N):
@@ -167,21 +162,24 @@
     heads = width // HEAD
 
     def own_columns():
-        bgv[...] = jnp.zeros_like(bgv)
-
-        def one(b, carry):
+        def one(b, sums):
             at = pl.ds(pl.multiple_of(b * rows, rows), rows)
+            new = []
             for h in range(heads):
                 value = (yl == 1) if h == heads - 1 else None
                 hs = pl.ds(h * HEAD, HEAD)
-                for line in range(2):
-                    r = turn_back(qb[b, line, :, hs].astype(f32), line, b, value)
-                    bgv[:, hs] += jnp.sum(r, axis=0, keepdims=True)
                 r = turn_back(qb[b, yl, :, hs].astype(f32), yl, b, value)
                 jl[at, pl.ds(pl.multiple_of(yl * width + h * HEAD, HEAD), HEAD)] = r.astype(bf16)
-            return carry
-
-        lax.fori_loop(0, Z, one, 0)
+                r = r + turn_back(qb[b, 1 - yl, :, hs].astype(f32), 1 - yl, b, value)
+                total = sums[h]
+                for q in range(rows // 8):
+                    total = total + r[q * 8:(q + 1) * 8]
+                new.append(total)
+            return tuple(new)
+
+        sums = lax.fori_loop(0, Z, one, (jnp.zeros((8, HEAD), f32),) * heads)
+        for h in range(heads):
+            bgv[:, h * HEAD:(h + 1) * HEAD] = jnp.sum(sums[h], axis=0, keepdims=True)
 
     def far_columns():
         def one(b, carry):
@@ -206,8 +204,8 @@
         lax.fori_loop(first, first + count, one, 0)
 
     def weights_here(c):
-        d_got(c, 0).wait_recv()
-        d_got(c, 1).wait_recv()
+        spot = w.at[w_rows(c, 0, 0, 0, 4), far]
+        rcopy(spot, spot, w_s.at[0], d_r.at[c], **sibling).wait_recv()
 
     def backward_chunk(c):
         weights_here(c)
@@ -217,7 +215,11 @@
         return pl.ds(pl.multiple_of(c * F + hf * H, H), H)
 
     def rs_copy(d, c, slot, src):
-        return rcopy(src, rb.at[d, c, slot], rs_s.at[d, c, slot], rs_r.at[d, c, slot], z=zz(1 if d == 0 else -1))
+        return rcopy(src, rb.at[d, c, slot], rs_s.at[0], rs_r.at[lax.rem(c, 4), slot], z=zz(1 if d == 0 else -1))
+
+    def rs_wait(c, slot):
+        spot = rb.at[:, c, slot]
+        rcopy(spot, spot, rs_s.at[0], rs_r.at[lax.rem(c, 4), slot], z=zz(1)).wait_recv()
 
     def first_hop(c):
         for d in range(2):
@@ -227,32 +229,23 @@
                 sb[d, c, short] = part[zz(dist if d == 0 else -dist), :, span(c, hf)].astype(bf16)
                 rs_copy(d, c, 4 * short, sb.at[d, c, short]).start()
 
-    def later_hop(c, hop):
-        def one(d, short):
-            hf = d if short == 0 else 1 - d
+    def pass_on(c, hop, short):
+        slot = 4 * short + hop - 1
+        rs_wait(c, slot)
+        for d in range(2):
+            hf = short if d == 0 else 1 - short
             dist = 4 - hop - short
-            slot = 4 * short + hop - 1
-            rs_copy(d, c, slot, rb.at[d, c, slot]).wait_recv()
             mine = part[zz(dist if d == 0 else -dist), :, span(c, hf)]
             rb[d, c, slot] = (rb[d, c, slot].astype(f32) + mine).astype(bf16)
             rs_copy(d, c, slot + 1, rb.at[d, c, slot]).start()
 
-        one(0, 0)
-        one(1, 0)
-
-        @pl.when(hop < 3)
-        def _():
-            one(0, 1)
-            one(1, 1)
-
     def ng_copy(c):
         at = pl.ds(pl.multiple_of(c * F, F), F)
-        return pltpu.make_async_copy(ng.at[:, at], ng_o.at[:, at], ng_s.at[c])
+        return pltpu.make_async_copy(ng.at[:, at], ng_o.at[:, at], ng_s.at[0])
 
     def finish(c):
-        for d in range(2):
-            rs_copy(d, c, 3, rb.at[d, c, 3]).wait_recv()
-            rs_copy(d, c, 6, rb.at[d, c, 6]).wait_recv()
+        rs_wait(c, 3)
+        rs_wait(c, 6)
         total = inner[...]
         for hf in range(2):
             at = span(c, hf)
@@ -266,25 +259,31 @@
 
     def gain_part(c):
         def one(t, carry):
+            per = H // 128
             at = pl.ds(pl.multiple_of(c * F + t * 128, 128), 128)
             total = jnp.zeros((rows, 128), f32)
             for b in range(Z):
                 total = total + part[b, :, at] * tok[b, :, at].astype(f32) * scl[b]
-            gp[c, :, pl.ds(pl.multiple_of(t * 128, 128), 128)] = jnp.sum(total, axis=0, keepdims=True)
+            spot = pl.ds(pl.multiple_of(lax.rem(t, per) * 128, 128), 128)
+            gp[c, t // per, :, spot] = jnp.sum(total, axis=0, keepdims=True)
             return carry
 
         lax.fori_loop(0, F // 128, one, 0)
 
+    def gy_send(c):
+        return rcopy(gp.at[c, 1 - yl], gy.at[c], gy_s.at[0], gy_r.at[0], **direct)
+
     def g_send(c):
-        return rcopy(gp.at[c], gr.at[z], g_s.at[c], g_r.at[z], z=c)
+        return rcopy(gp.at[c, yl], gr.at[z], g_s.at[0], g_r.at[0], z=c)
 
     def gf_send(k):
-        return rcopy(gf.at[z], gf.at[z], gf_s.at[k], gf_r.at[z], z=zz(k))
-
-    gy_copy = rcopy(gs, gy, gy_s.at[0], gy_r.at[0], **direct)
+        return rcopy(gf.at[yl, z], gf.at[yl, z], gf_s.at[0], gf_r.at[0], z=zz(k))
+
+    gl_copy = rcopy(gf.at[yl], gf.at[yl], gl_s.at[0], gl_r.at[0], **direct)
+    g_out = [pltpu.make_async_copy(gf.at[h], gg_o.at[:, h], loc.at[10 + h]) for h in range(2)]
 
     def forward_quarter(t, k):
-        n = jnp.where(yl == 0, 4 - t, t)
+        n = jnp.where(yl == 0, t, 4 - t)
         cols = pl.ds(pl.multiple_of(n * 256, 256), 256)
         deep = dim // 4
 
@@ -296,24 +295,26 @@
         lhs = nrm[:, :, at].reshape(Z * rows, deep)
         acc[...] += jnp.dot(lhs, w[at, cols], preferred_element_type=f32)
 
-        def spin(b, carry):
-            at = pl.ds(pl.multiple_of(b * rows, rows), rows)
-            for h in range(2):
-                x = acc[at, h * HEAD:(h + 1) * HEAD]
-                r = x * cosv[yl, at, :] + pltpu.roll(x, HEAD // 2, 1) * sinv[yl, at, :]
-                if h == 1:
-                    r = jnp.where(n == 4, x, r)
-                out[b, :, pl.ds(pl.multiple_of(n * 256 + h * HEAD, HEAD), HEAD)] = r.astype(bf16)
-            return carry
-
         @pl.when(k == 3)
         def _():
-            lax.fori_loop(0, Z, spin, 0)
-
-    o_copy = rcopy(out.at[:, :, far], qkv_o.at[:, yl], o_s.at[0], o_r.at[0], **direct)
+            for b in range(Z):
+                at = pl.ds(b * rows, rows)
+                for h in range(2):
+                    x = acc[at, h * HEAD:(h + 1) * HEAD]
+                    r = x * cosv[yl, at, :] + pltpu.roll(x, HEAD // 2, 1) * sinv[yl, at, :]
+                    if h == 1:
+                        r = jnp.where(n == 4, x, r)
+                    out[b, :, pl.ds(pl.multiple_of(n * 256 + h * HEAD, HEAD), HEAD)] = r.astype(bf16)
+
+    def o_copy(p):
+        start = ((width, width - 128), (width + 128, 256), (width + 384, 0))[p]
+        n = 128 if p == 0 else 256
+        src = pl.multiple_of(jnp.where(yl == 0, start[0], start[1]), 128)
+        dst = pl.multiple_of(src - (1 - yl) * width, 128)
+        return rcopy(out.at[:, :, pl.ds(src, n)], qkv_o.at[:, yl, :, pl.ds(dst, n)], o_s.at[0], o_r.at[0], **direct)
+
     o_local = pltpu.make_async_copy(out.at[:, :, own], qkv_o.at[:, yl], loc.at[8])
 
-    g_out = pltpu.make_async_copy(gf, gg_o, loc.at[10])
     inner[...] = jnp.zeros_like(inner)
 
     for k in range(1, 5):
@@ -326,11 +327,8 @@
     bg_copy.start()
 
     for k in range(PER):
+        rcopy(tok.at[z], tok.at[z], ag_s.at[0], ag_r.at[k], z=zz(1)).wait_recv()
         for d in range(2):
-            block = zz(-1 - k // 2) if d == 0 else zz(1 + k // 2)
-            cols = pl.ds(ag_half(d, k) * half, half)
-            spot = tok.at[block, :, cols]
-            rcopy(spot, spot, ag_s.at[d, k], ag_r.at[d, k], z=zz(1)).wait_recv()
             if k + 2 < PER:
                 ag_copy(d, k + 2).start()
         for j in {1: (0,), 2: (1, 2), 3: (3, 4), 4: (5,), 5: (6, 7)}.get(k, ()):
@@ -343,128 +341,123 @@
             bias[:, own] = b_own[...].reshape(1, width)
             bias[:, far] = b_far[...].reshape(1, width)
             far_columns()
-        if k in (1, 3):
+        if k == 4:
+            local[6].wait()
+            for c in range(3):
+                backward_chunk(c)
+        if k == 5:
+            for c in range(3):
+                first_hop(c)
+        if k in (1, 3, 5):
             norm_block(zz(-1 - k // 2))
             norm_block(zz(1 + k // 2))
-        if k == 4:
-            local[6].wait()
-            backward_chunk(0)
         if k == 5:
-            first_hop(0)
-            backward_chunk(1)
-            first_hop(1)
-            norm_block(zz(-3))
-            norm_block(zz(3))
-            backward_chunk(2)
-            first_hop(2)
-        if k == 6:
             backward_chunk(3)
             first_hop(3)
+            backward_chunk(4)
+        if k == 6:
             norm_block(zz(4))
 
     def event(e, carry):
         r = lax.rem(e, 16)
+        base = e // 16 * 4
         hop = r // 4
-        c = e // 16 * 4 + lax.rem(r, 4)
+        c = base + lax.rem(r, 4)
 
         @pl.when((hop == 0) & (e < 32))
         def _():
             first_hop(c)
 
-        @pl.when((hop > 0) & (e < 32))
-        def _():
-            later_hop(c, hop)
-
-        @pl.when((e == 5) | (e == 7))
-        def _():
-            hand_over(6 + (e - 5) // 2)
-
-        @pl.when(e < 12)
-        def _():
-            c = 4 + (e - 4) // 2
-            odd = lax.rem(e, 2)
+        @pl.when(hop > 0)
+        def _():
+            j = lax.rem(r, 4)
+            pair = base + 2 * lax.rem(j, 2)
+            pass_on(jnp.where(hop == 2, pair, c), hop, jnp.where(hop == 2, j // 2, 0))
+
+            @pl.when(hop < 3)
+            def _():
+                pass_on(jnp.where(hop == 2, pair + 1, c), hop, jnp.where(hop == 2, j // 2, 1))
+
+        @pl.when((e == 4) | (e == 6))
+        def _():
+            hand_over(6 + (e - 4) // 2)
+
+        @pl.when((e >= 5) & (e < 11))
+        def _():
+            c = 5 + (e - 5) // 2
+            odd = lax.rem(e - 5, 2)
 
             @pl.when(odd == 0)
             def _():
                 weights_here(c)
             backward_part(c, odd * (F // bt // 2), F // bt // 2)
 
-        @pl.when((e >= 8) & (e < 16))
-        def _():
-            c = e - 8
+        @pl.when((e < 9) | ((e >= 11) & (e < 14)))
+        def _():
+            c = jnp.where(e < 9, e - 4, e - 6)
             gain_part(c)
-
-            @pl.when(c != z)
-            def _():
-                g_send(c).start()
-
-        @pl.when((e >= 12) & (e < 32))
-        def _():
-            forward_quarter((e - 12) // 4, lax.rem(e, 4))
-
-        @pl.when(e == 21)
-        def _():
-            total = gp[z]
+            gy_send(c).start()
+
+        @pl.when(e == 17)
+        def _():
+            rcopy(gy, gy, gy_s.at[0], gy_r.at[0], **direct).wait()
+            for c in range(N):
+                gp[c, yl] = gp[c, yl] + gy[c]
+
+                @pl.when(c != z)
+                def _(c=c):
+                    g_send(c).start()
+
+        @pl.when((e >= 9) & (e < 29))
+        def _():
+            forward_quarter((e - 9) // 4, lax.rem(e - 9, 4))
+
+        for p, when in enumerate((20, 24, 28)):
+            @pl.when(e == when)
+            def _(p=p):
+                o_copy(p).start()
+
+        @pl.when(e == 24)
+        def _():
+            total = gp[z, yl]
+            spot = gr.at[pl.ds(0, Z - 1)]
+            rcopy(spot, spot, g_s.at[0], g_r.at[0], z=zz(1)).wait()
             for k in range(1, Z):
-                spot = gr.at[zz(k)]
-                rcopy(spot, spot, g_s.at[zz(k)], g_r.at[zz(k)], z=zz(1)).wait_recv()
                 total = total + gr[zz(k)]
-            gs[...] = total
-            gy_copy.start()
-
-        @pl.when(e == 24)
-        def _():
-            o_copy.start()
-
-        @pl.when(e == 25)
-        def _():
-            gy_copy.wait_recv()
-            gf[z] = gs[...] + gy[...]
+            gf[yl, z] = total
             for k in range(1, Z):
                 gf_send(k).start()
 
-        @pl.when((e >= 24) & (e < 32))
-        def _():
-            c = e - 24
-            for k in range(2):
-                w_copy(c, k).wait_send()
-                x_copy(c, k).wait_send()
-                d_copy(c, k).wait_send()
-
-            @pl.when(c != z)
-            def _():
-                g_send(c).wait_send()
-
-        @pl.when(e >= 28)
-        def _():
-            c = e - 28
-            for d in range(2):
-                for slot in range(PER):
-                    rs_copy(d, c, slot, rb.at[d, c, slot]).wait_send()
-
-        @pl.when(e == 28)
-        def _():
-            for d in range(2):
-                for k in range(PER):
-                    ag_copy(d, k).wait_send()
+        @pl.when(e == 29)
+        def _():
+            spot = gf.at[0, pl.ds(0, Z - 1)]
+            rcopy(spot, spot, gf_s.at[0], gf_r.at[0], z=zz(1)).wait()
+            gl_copy.start()
+
+        @pl.when(e == 32)
+        def _():
+            o_local.start()
+
+        @pl.when(((e >= 18) & (e < 22)) | (e >= 32))
+        def _():
+            finish(jnp.where(e < 22, e - 18, e - 28))
+
+        @pl.when(e == 25)
+        def _():
+            spot = tok.at[pl.ds(0, PER)]
+            rcopy(spot, spot, ag_s.at[0], ag_r.at[0], z=zz(1)).wait_send()
             q_copy.wait_send()
             b_copy.wait_send()
-            gy_copy.wait_send()
-
-        @pl.when(e == 32)
-        def _():
-            o_local.start()
+            spot = w.at[:, own]
+            rcopy(spot, spot, w_s.at[0], w_r.at[0], **direct).wait_send()
 
         @pl.when(e == 33)
         def _():
-            for k in range(1, Z):
-                spot = gf.at[zz(k)]
-                rcopy(spot, spot, gf_s.at[k], gf_r.at[zz(k)], z=zz(1)).wait_recv()
-            g_out.start()
-
-        @pl.when(((e >= 24) & (e < 28)) | (e >= 32))
-        def _():
-            finish(jnp.where(e < 28, e - 24, e - 28))
+            gl_copy.wait_send()
+            spot = gf.at[1 - yl]
+            rcopy(spot, spot, gl_s.at[0], gl_r.at[0], **direct).wait_recv()
+            for h in range(2):
+                g_out[h].start()
         return carry
 
     lax.fori_loop(4, 36, event, 0)
@@ -474,14 +467,13 @@
     st[1] = s * s * s * jnp.broadcast_to(mean, s.shape)
     st_copy = pltpu.make_async_copy(st, st_o, loc.at[9])
     st_copy.start()
-    for k in range(1, Z):
-        gf_send(k).wait_send()
     bg_copy.wait()
-    o_copy.wait()
+    rcopy(out.at[:, :, far], out.at[:, :, far], o_s.at[0], o_r.at[0], **direct).wait()
+    rcopy(rb, rb, rs_s.at[0], rs_r.at[0, 0], z=zz(1)).wait_send()
     o_local.wait()
-    g_out.wait()
-    for c in range(N):
-        ng_copy(c).wait()
+    for h in range(2):
+        g_out[h].wait()
+    pltpu.make_async_copy(ng, ng_o, ng_s.at[0]).wait()
     st_copy.wait()
 
 
@@ -577,7 +569,7 @@
             jax.ShapeDtypeStruct((Z, 2, rows, width), bf16),
             jax.ShapeDtypeStruct((rows, dim), f32),
             jax.ShapeDtypeStruct((2, rows, 128), f32),
-            jax.ShapeDtypeStruct((Z, 1, F), f32),
+            jax.ShapeDtypeStruct((Z, 2, 1, H), f32),
             jax.ShapeDtypeStruct((width,), f32),
         ),
         in_specs=[any_spec] * 7,
@@ -598,11 +590,10 @@
             V((Z, rows, 128), f32),
             V((rows, 128), f32),
             V((Z * rows, 256), f32),
-            V((N, 1, F), f32),
-            V((Z, 1, F), f32),
-            V((1, F), f32),
-            V((1, F), f32),
-            V((Z, 1, F), f32),
+            V((N, 2, 1, H), f32),
+            V((Z, 1, H), f32),
+            V((N, 1, H), f32),
+            V((2, Z, 1, H), f32),
             V((1, dim), f32),
             V((1, both), f32),
             V((width,), f32),
@@ -611,18 +602,17 @@
             V((width,), f32),
             V(cos.shape, f32),
             V(sin.shape, f32),
-            dma((2, PER)), dma((2, PER)),
-            dma((2, N)), dma((2, N)),
-            dma((2, N)), dma((2, N)),
-            dma((2, N)), dma((2, N)),
-            dma((2, N, PER)), dma((2, N, PER)),
+            dma((PER,)), dma((1,)),
+            dma((N,)), dma((1,)), dma((N,)), dma((N,)),
+            dma((4, PER)), dma((1,)),
             dma((1,)), dma((1,)),
             dma((1,)), dma((1,)),
             dma((1,)), dma((1,)),
-            dma((Z,)), dma((Z,)),
             dma((1,)), dma((1,)),
-            dma((Z,)), dma((Z,)),
-            dma((N,)),
+            dma((1,)), dma((1,)),
+            dma((1,)), dma((1,)),
+            dma((1,)), dma((1,)),
+            dma((1,)),
             dma((14,)),
         ],
         compiler_params=pltpu.CompilerParams(
@@ -643,7 +633,7 @@
         out_shape=(
             jax.ShapeDtypeStruct((Z, 2, rows, width), bf16),
             jax.ShapeDtypeStruct((rows, dim), f32),
-            jax.ShapeDtypeStruct((Z, 1, F), f32),
+            jax.ShapeDtypeStruct((Z, 2, 1, H), f32),
             jax.ShapeDtypeStruct((width,), f32),
         ),
         in_specs=[any_spec] * 7,
@@ -652,7 +642,7 @@
             V((Z, 2, rows, width), bf16),
             V((rows, dim), f32),
             V((2, rows, 128), f32),
-            V((Z, 1, F), f32),
+            V((Z, 2, 1, H), f32),
             V((width,), f32),
             V((rows, dim), bf16),
             V((1, dim), f32),

time: 99 us -> 94.5 us (0.955)
  Pallas kernels: 98.2 us -> 93.8 us
    pallas_call x1, Pallas kernels: 95.7 us -> 91.2 us  [shards(): pl.pallas_call(kernel, name='qkv_ring', out_shape=(jax.ShapeDtypeStruct((...]
where the time goes in v4:
time: 94.5 us; the launch traced here: 94.4 us
  Pallas kernels  93.8 us (99%)
    pallas_call x1, Pallas kernels, shards(): pl.pallas_call(kernel, name='qkv_ring', out_shape=(jax.ShapeDtypeStruct((...  91.2 us
    pallas_call x1, Pallas kernels, shards(): pl.pallas_call(settle, name='settle', out_shape=(jax.ShapeDtypeStruct((Z,...  2.57 us

profile of v4, /device:TPU:4, one launch (start us, length us, event | category | flops | bytes accessed | tf_op | source)
XLA Modules:
  0.0 94.4 jit_solution(4446068687820240107)
XLA Ops:
  0.6 91.2 %qkv_ring.1 = (bf16[8,2,32,640]{3,2,1,0:T(8,128)(2,1)}, f32[32,8192]{1,0:T(8,128)}, f32[2,32,128]{2,1,0:T(8,128)}, f32[8,2,1,512]{3,2,1,0:T(1,128)}, f32[640]{0:T(1024)}) custom-call(bf16[32,8192]{1,0:T(8,128)(2,1)} %tok_h.3, bf16[8192,640]{1,0:T(8,128)(2,1)} %w_h.1, bf16[8,2,32,640]{3,2,1,0:T(8,128)(2,1)} %bitcast.4, f32[1,8192]{1,0:T(1,128)} %bitcast.5, ...), custom_call_target="tpu_custom_call" | custom-call | tf_op jit(solution)/shard_map/qkv_ring/pallas_call | solution.py:565
  91.9 2.6 %settle.1 = (bf16[8,2,32,640]{3,2,1,0:T(8,128)(2,1)}, f32[32,8192]{1,0:T(8,128)}, f32[8,2,1,512]{3,2,1,0:T(1,128)}, f32[640]{0:T(1024)}) custom-call(bf16[8,2,32,640]{3,2,1,0:T(8,128)(2,1)} %get-tuple-element.13.qkv_i, f32[32,8192]{1,0:T(8,128)} %get-tuple-element.14.ng_i, f32[2,32,128]{2,1,0:T(8,128)} %get-tuple-element.15.st_i, ...), custom_call_target="tpu_custom_call" | custom-call | tf_op jit(solution)/shard_map/settle/pallas_call | solution.py:630

commit v5 on v4

--- a/solution.py
+++ b/solution.py
@@ -86,14 +86,17 @@
             ag_copy(d, k).start()
 
     q_copy = rcopy(qg_h.at[:, 1 - yl], qp, q_s.at[0], q_r.at[0], **direct)
-    q_copy.start()
     b_copy = rcopy(bias_h, b_far, b_s.at[0], b_r.at[0], **direct)
-    b_copy.start()
 
     piece = F // 8
 
+    cut = 7 * piece // 8
+
     def w_rows(j, par, who, s, n):
-        return pl.ds(pl.multiple_of(j * F + par * 4 * piece + who * 2 * piece + s * piece, piece), n * piece)
+        first = j * F + par * 4 * piece + who * 2 * piece
+        if n > 1:
+            return pl.ds(pl.multiple_of(first, 2 * piece), n * piece)
+        return pl.ds(pl.multiple_of(first + s * cut, 16), cut if s == 0 else 2 * piece - cut)
 
     def w_copy(j, s):
         at = w_rows(j, side, core, s, 1)
@@ -104,7 +107,7 @@
         return rcopy(spot, spot, w_s.at[0], w_r.at[j], **direct)
 
     def x_copy(j, s):
-        spot = w.at[w_rows(j, side, core, s, 1), far]
+        spot = w.at[w_rows(j, side, core, 0, 2), far].at[pl.ds(s * piece, piece)]
         return rcopy(spot, spot, w_s.at[0], x_r.at[j], **beside[s])
 
     def x_got(j):
@@ -126,6 +129,9 @@
         d_copy(j, 1).start()
 
     for j in range(N):
+        if j == 4:
+            b_copy.start()
+            q_copy.start()
         w_copy(j, 0).start()
         w_copy(j, 1).start()
 
@@ -331,29 +337,32 @@
         for d in range(2):
             if k + 2 < PER:
                 ag_copy(d, k + 2).start()
-        for j in {1: (0,), 2: (1, 2), 3: (3, 4), 4: (5,), 5: (6, 7)}.get(k, ()):
+        for j in {1: (0, 1), 2: (2, 3), 3: (4,), 4: (5, 6), 5: (7,)}.get(k, ()):
             hand_on(j)
-        for j in {3: (0,), 4: (1, 2), 5: (3, 4), 6: (5,)}.get(k, ()):
+        for j in {3: (0, 1), 4: (2,), 6: (6,)}.get(k, ()):
             hand_over(j)
-        if k == 1:
+        if k == 2:
             q_copy.wait_recv()
             b_copy.wait_recv()
             bias[:, own] = b_own[...].reshape(1, width)
             bias[:, far] = b_far[...].reshape(1, width)
             far_columns()
-        if k == 4:
             local[6].wait()
-            for c in range(3):
-                backward_chunk(c)
         if k == 5:
             for c in range(3):
                 first_hop(c)
         if k in (1, 3, 5):
             norm_block(zz(-1 - k // 2))
             norm_block(zz(1 + k // 2))
+        if k == 4:
+            for c in range(3):
+                backward_chunk(c)
+            hand_over(3)
+            hand_over(4)
         if k == 5:
             backward_chunk(3)
             first_hop(3)
+            hand_over(5)
             backward_chunk(4)
         if k == 6:
             norm_block(zz(4))
@@ -378,27 +387,27 @@
             def _():
                 pass_on(jnp.where(hop == 2, pair + 1, c), hop, jnp.where(hop == 2, j // 2, 1))
 
-        @pl.when((e == 4) | (e == 6))
-        def _():
-            hand_over(6 + (e - 4) // 2)
-
-        @pl.when((e >= 5) & (e < 11))
-        def _():
-            c = 5 + (e - 5) // 2
-            odd = lax.rem(e - 5, 2)
+        @pl.when(e == 5)
+        def _():
+            hand_over(7)
+
+        @pl.when(e < 10)
+        def _():
+            c = 5 + (e - 4) // 2
+            odd = lax.rem(e, 2)
 
             @pl.when(odd == 0)
             def _():
                 weights_here(c)
             backward_part(c, odd * (F // bt // 2), F // bt // 2)
 
-        @pl.when((e < 9) | ((e >= 11) & (e < 14)))
-        def _():
-            c = jnp.where(e < 9, e - 4, e - 6)
+        @pl.when(e < 12)
+        def _():
+            c = e - 4
             gain_part(c)
             gy_send(c).start()
 
-        @pl.when(e == 17)
+        @pl.when(e == 16)
         def _():
             rcopy(gy, gy, gy_s.at[0], gy_r.at[0], **direct).wait()
             for c in range(N):
@@ -408,16 +417,22 @@
                 def _(c=c):
                     g_send(c).start()
 
-        @pl.when((e >= 9) & (e < 29))
-        def _():
-            forward_quarter((e - 9) // 4, lax.rem(e - 9, 4))
+        @pl.when(((e >= 10) & (e < 12)) | ((e >= 16) & (e < 28)))
+        def _():
+            q = jnp.where(e < 12, e - 10, jnp.where(e < 22, 2 * e - 30, e - 8))
+            forward_quarter(q // 4, lax.rem(q, 4))
+
+        @pl.when((e >= 16) & (e < 22))
+        def _():
+            q = 2 * e - 29
+            forward_quarter(q // 4, lax.rem(q, 4))
 
         for p, when in enumerate((20, 24, 28)):
             @pl.when(e == when)
             def _(p=p):
                 o_copy(p).start()
 
-        @pl.when(e == 24)
+        @pl.when(e == 21)
         def _():
             total = gp[z, yl]
             spot = gr.at[pl.ds(0, Z - 1)]
@@ -428,7 +443,7 @@
             for k in range(1, Z):
                 gf_send(k).start()
 
-        @pl.when(e == 29)
+        @pl.when(e == 26)
         def _():
             spot = gf.at[0, pl.ds(0, Z - 1)]
             rcopy(spot, spot, gf_s.at[0], gf_r.at[0], z=zz(1)).wait()

time: 94.5 us -> 93.7 us (level)
  no operation moved by 1% of the time
where the time goes in v5:
time: 93.7 us; the launch traced here: 93.6 us
  Pallas kernels  93 us (99%)
    pallas_call x1, Pallas kernels, shards(): pl.pallas_call(kernel, name='qkv_ring', out_shape=(jax.ShapeDtypeStruct((...  90.4 us
    pallas_call x1, Pallas kernels, shards(): pl.pallas_call(settle, name='settle', out_shape=(jax.ShapeDtypeStruct((Z,...  2.57 us

profile of v5, /device:TPU:4, one launch (start us, length us, event | category | flops | bytes accessed | tf_op | source)
XLA Modules:
  0.0 93.6 jit_solution(10797032516733801780)
XLA Ops:
  0.6 90.4 %qkv_ring.1 = (bf16[8,2,32,640]{3,2,1,0:T(8,128)(2,1)}, f32[32,8192]{1,0:T(8,128)}, f32[2,32,128]{2,1,0:T(8,128)}, f32[8,2,1,512]{3,2,1,0:T(1,128)}, f32[640]{0:T(1024)}) custom-call(bf16[32,8192]{1,0:T(8,128)(2,1)} %tok_h.3, bf16[8192,640]{1,0:T(8,128)(2,1)} %w_h.1, bf16[8,2,32,640]{3,2,1,0:T(8,128)(2,1)} %bitcast.4, f32[1,8192]{1,0:T(1,128)} %bitcast.5, ...), custom_call_target="tpu_custom_call" | custom-call | tf_op jit(solution)/shard_map/qkv_ring/pallas_call | solution.py:580
  91.0 2.6 %settle.1 = (bf16[8,2,32,640]{3,2,1,0:T(8,128)(2,1)}, f32[32,8192]{1,0:T(8,128)}, f32[8,2,1,512]{3,2,1,0:T(1,128)}, f32[640]{0:T(1024)}) custom-call(bf16[8,2,32,640]{3,2,1,0:T(8,128)(2,1)} %get-tuple-element.13.qkv_i, f32[32,8192]{1,0:T(8,128)} %get-tuple-element.14.ng_i, f32[2,32,128]{2,1,0:T(8,128)} %get-tuple-element.15.st_i, ...), custom_call_target="tpu_custom_call" | custom-call | tf_op jit(solution)/shard_map/settle/pallas_call | solution.py:645

commit v6 on v5

--- a/solution.py
+++ b/solution.py
@@ -221,7 +221,8 @@
         return pl.ds(pl.multiple_of(c * F + hf * H, H), H)
 
     def rs_copy(d, c, slot, src):
-        return rcopy(src, rb.at[d, c, slot], rs_s.at[0], rs_r.at[lax.rem(c, 4), slot], z=zz(1 if d == 0 else -1))
+        got = jnp.where(slot == 6, 3, slot)
+        return rcopy(src, rb.at[d, c, slot], rs_s.at[0], rs_r.at[lax.rem(c, 4), got], z=zz(1 if d == 0 else -1))
 
     def rs_wait(c, slot):
         spot = rb.at[:, c, slot]
@@ -250,8 +251,8 @@
         return pltpu.make_async_copy(ng.at[:, at], ng_o.at[:, at], ng_s.at[0])
 
     def finish(c):
-        rs_wait(c, 3)
-        rs_wait(c, 6)
+        spot = rb.at[:, c, pl.ds(3, 2)]
+        rcopy(spot, spot, rs_s.at[0], rs_r.at[lax.rem(c, 4), 3], z=zz(1)).wait_recv()
         total = inner[...]
         for hf in range(2):
             at = span(c, hf)
@@ -541,15 +542,15 @@
 
         lax.fori_loop(0, wide // step, one, 0)
         at = pl.ds(q * wide, wide)
-        copy = pltpu.make_async_copy(ng.at[:, at], tg_o.at[:, at], tg_s.at[q])
+        copy = pltpu.make_async_copy(ng.at[:, at], tg_o.at[:, at], tg_s.at[0])
         copy.start()
-        sent.append(copy)
         got, put = through[q]
         got.wait()
         put.start()
         sent.append(put)
     for copy in sent:
         copy.wait()
+    pltpu.make_async_copy(ng, tg_o, tg_s.at[0]).wait()
 
 
 def tables(tokens_per):
@@ -619,7 +620,7 @@
             V(sin.shape, f32),
             dma((PER,)), dma((1,)),
             dma((N,)), dma((1,)), dma((N,)), dma((N,)),
-            dma((4, PER)), dma((1,)),
+            dma((4, PER - 1)), dma((1,)),
             dma((1,)), dma((1,)),
             dma((1,)), dma((1,)),
             dma((1,)), dma((1,)),
@@ -628,7 +629,7 @@
             dma((1,)), dma((1,)),
             dma((1,)), dma((1,)),
             dma((1,)),
-            dma((14,)),
+            dma((12,)),
         ],
         compiler_params=pltpu.CompilerParams(
             collective_id=0, has_side_effects=True, vmem_limit_bytes=66_000_000
@@ -661,7 +662,7 @@
             V((width,), f32),
             V((rows, dim), bf16),
             V((1, dim), f32),
-            dma((7,)), dma((4,)), dma((4,)), dma((4,)),
+            dma((7,)), dma((4,)), dma((4,)), dma((1,)),
         ],
         compiler_params=pltpu.CompilerParams(vmem_limit_bytes=66_000_000),
     )(*raw, tokens, norm_gain.reshape(1, dim))

time: 93.7 us -> 93.6 us (level)
  no operation moved by 1% of the time
where the time goes in v6:
time: 93.6 us; the launch traced here: 93.5 us
  Pallas kernels  92.9 us (99%)
    pallas_call x1, Pallas kernels, shards(): pl.pallas_call(kernel, name='qkv_ring', out_shape=(jax.ShapeDtypeStruct((...  90.3 us
    pallas_call x1, Pallas kernels, shards(): pl.pallas_call(settle, name='settle', out_shape=(jax.ShapeDtypeStruct((Z,...  2.54 us

profile of v6, /device:TPU:4, one launch (start us, length us, event | category | flops | bytes accessed | tf_op | source)
XLA Modules:
  0.0 93.5 jit_solution(4896006482835478868)
XLA Ops:
  0.6 90.3 %qkv_ring.1 = (bf16[8,2,32,640]{3,2,1,0:T(8,128)(2,1)}, f32[32,8192]{1,0:T(8,128)}, f32[2,32,128]{2,1,0:T(8,128)}, f32[8,2,1,512]{3,2,1,0:T(1,128)}, f32[640]{0:T(1024)}) custom-call(bf16[32,8192]{1,0:T(8,128)(2,1)} %tok_h.3, bf16[8192,640]{1,0:T(8,128)(2,1)} %w_h.1, bf16[8,2,32,640]{3,2,1,0:T(8,128)(2,1)} %bitcast.4, f32[1,8192]{1,0:T(1,128)} %bitcast.5, ...), custom_call_target="tpu_custom_call" | custom-call | tf_op jit(solution)/shard_map/qkv_ring/pallas_call | solution.py:581
  91.0 2.5 %settle.1 = (bf16[8,2,32,640]{3,2,1,0:T(8,128)(2,1)}, f32[32,8192]{1,0:T(8,128)}, f32[8,2,1,512]{3,2,1,0:T(1,128)}, f32[640]{0:T(1024)}) custom-call(bf16[8,2,32,640]{3,2,1,0:T(8,128)(2,1)} %get-tuple-element.13.qkv_i, f32[32,8192]{1,0:T(8,128)} %get-tuple-element.14.ng_i, f32[2,32,128]{2,1,0:T(8,128)} %get-tuple-element.15.st_i, ...), custom_call_target="tpu_custom_call" | custom-call | tf_op jit(solution)/shard_map/settle/pallas_call | solution.py:646
